TPU v7x, 256 devices: a whole 4x4x8 slice. The times are simulated.
256 devices in a mesh: solver: 64 (over y, x, z_lo, core), group: 4 (over z_hi).
Axes of the slice: x: 4, y: 4, z: 8 (z_hi: 4, z_lo: 2; z = z_hi * 2 + z_lo), core: 2. Of those that a mesh axis runs over, the one named last changes fastest.
Arguments:
- field: float32 [8, 8, 8, 65536], P(None, None, None, ('solver', 'group')), may hold values from -6 to 6
- first_weight: bfloat16 [8, 1024], replicated, may hold values from -2 to 2
- second_weight: bfloat16 [1024, 1], replicated, may hold values from -0.1875 to 0.1875
- face_edges: int32 [2, 256], replicated, may hold values from 0 to 63, as said below
- sample_index: int32 [16384], P(('solver', 'group')), may hold values from 0 to 31
- route: int32 [16384, 1], P(('solver', 'group')), may hold values from 0 to 63; in each aligned block of 64 rows (0 to 63, 64 to 127, ...) at most 2 rows name the same one
Outputs:
- new_field: float32 [8, 8, 8, 65536], P(None, None, None, ('solver', 'group'))
- new_first: bfloat16 [8, 1024], replicated
- new_second: bfloat16 [1024, 1], replicated
Inputs may be any that keep to these rules, and one draw needn't show every extreme that they name: `sample_index`: indices of wall elements (ey = 0) of the sample's own device, in the order ex * 8 + ez; they may repeat. `route`: at most 2 of the samples of one device name one learner, a bound that some block reaches by some device in every draw. `face_edges`: no edge joins a node to itself; edges may repeat.
All inputs are finite; a program needn't handle non-finite values.
Results may differ from a plain program's by a relative error of at most 0.001.
The roundings to bfloat16 on the way count: a program that leaves them out, or rounds other values in their place, can miss the bound.
Values sent between devices are 32-bit elements; how exact they have to be, the bound alone decides.
No kernel may reach another device: no remote copies, remote signals or barrier semaphores. Data moves between devices by JAX's collectives and lax.ppermute only.
A program may use at most 128 MiB of HBM per device.

v0:
```python
import math

import jax
import jax.numpy as jnp
import numpy as np
from jax import lax
from jax.experimental import pallas as pl
from jax.experimental.pallas import tpu as pltpu
from jax.sharding import PartitionSpec as P


FLOW_STEPS = 5
EXL = 4
EY = 8
POINTS = 8
HID = 1024
TIME_STEP = 0.002
VISCOSITY = 0.01
VELOCITY = 1.0
PENALTY = 1.0
STRESS_SCALE = 0.1
LEARN_RATE = 0.05


BF = jnp.bfloat16
F32 = jnp.float32


def legendre_table(points_x, points):
    table = np.zeros((points_x.shape[0], points))
    table[:, 0] = 1.0
    table[:, 1] = points_x
    for degree in range(2, points):
        table[:, degree] = (
            (2 * degree - 1) * points_x * table[:, degree - 1] - (degree - 1) * table[:, degree - 2]
        ) / degree
    return table


def gll_tables(points):
    order = points - 1
    guess = np.cos(np.pi * np.arange(points) / order)
    for _ in range(100):
        table = legendre_table(guess, points)
        guess = guess - (guess * table[:, order] - table[:, order - 1]) / (points * table[:, order])
    nodes = guess[::-1]
    values = legendre_table(nodes, points)[:, order]
    matrix = np.zeros((points, points))
    for row in range(points):
        for column in range(points):
            if row != column:
                matrix[row, column] = values[row] / (values[column] * (nodes[row] - nodes[column]))
    matrix[0, 0] = -order * (order + 1) / 4.0
    matrix[order, order] = order * (order + 1) / 4.0
    return matrix, 2.0 / (order * (order + 1))


DERIV, END_WEIGHT = gll_tables(POINTS)
GAIN = 2.0 / END_WEIGHT
PEN = TIME_STEP * GAIN * PENALTY
PEN_IN = TIME_STEP * GAIN * (VELOCITY + PENALTY)


def flow_constants():
    second = DERIV @ DERIV
    along_x = TIME_STEP * (-2.0 * VELOCITY * DERIV + 4.0 * VISCOSITY * second)
    along_x[0, 0] -= PEN_IN
    along_x[7, 7] -= PEN
    across = TIME_STEP * 4.0 * VISCOSITY * second
    across[0, 0] -= PEN
    across[7, 7] -= PEN
    eye = np.eye(8)
    volume = np.kron(np.eye(4), np.kron(across, eye) + np.kron(eye, across))
    plane = np.eye(64) + np.kron(along_x, eye) + np.kron(eye, across)
    normal = np.zeros((64, 64))
    for ey in range(EY):
        block = across.copy()
        if ey == 0:
            block[0, 0] += PEN
        normal[ey * 8 : ey * 8 + 8, ey * 8 : ey * 8 + 8] = block
        if ey > 0:
            normal[ey * 8, ey * 8 - 1] += PEN
        if ey < EY - 1:
            normal[ey * 8 + 7, ey * 8 + 8] += PEN
    source = np.zeros((64,))
    source[0] = TIME_STEP * GAIN
    powers = [source]
    for _ in range(FLOW_STEPS - 1):
        powers.append(normal @ powers[-1])
    columns = np.zeros((FLOW_STEPS * 8, 256))
    for p in range(FLOW_STEPS):
        total = sum(math.comb(m, p) * powers[m - p] for m in range(p, FLOW_STEPS))
        for j in range(8):
            for lane in range(256):
                columns[p * 8 + j, lane] = total[(lane % 8) * 8 + j]
    return along_x, volume, plane, columns


def halves(table):
    high = np.asarray(table, np.float32).astype(BF)
    low = (table - high.astype(np.float64)).astype(np.float32).astype(BF)
    return high, low


ALONG_X, VOLUME, PLANE, COLUMNS = flow_constants()
VOLUME_HIGH, VOLUME_LOW = halves(VOLUME)
PLANE_HIGH, PLANE_LOW = halves(PLANE)


def two(value):
    high = value.astype(BF)
    return high, (value - high.astype(F32)).astype(BF)


def three(value):
    high = value.astype(BF)
    rest = value - high.astype(F32)
    middle = rest.astype(BF)
    return high, middle, (rest - middle.astype(F32)).astype(BF)


def dot(a, b):
    return jnp.dot(a, b, preferred_element_type=F32)


def dot_t(a, b):
    return lax.dot_general(a, b, (((1,), (1,)), ((), ())), preferred_element_type=F32)


def lanes(shape):
    return lax.broadcasted_iota(jnp.int32, shape, len(shape) - 1)


def rows(shape):
    return lax.broadcasted_iota(jnp.int32, shape, len(shape) - 2)


def roll(value, shift):
    size = value.shape[-1]
    shift = shift % size
    return value if shift == 0 else pltpu.roll(value, shift, value.ndim - 1)


def exact_dot(table, value):
    a, b, c = three(value)
    return dot(table, a) + dot(table, b) + dot(table, c)


def start_kernel(parity, field_far, route_far, counts, near, far, field, route, sems):
    copies = [
        pltpu.make_async_copy(route_far, route, sems.at[0]),
        pltpu.make_async_copy(field_far, field, sems.at[1]),
    ]
    for copy in copies:
        copy.start()
    copies[0].wait()
    learner = lax.broadcasted_iota(jnp.int32, (128, 64), 0)
    hits = (learner == route[...]).astype(BF)
    counts[...] = dot_t(jnp.ones((64, 64), BF), hits)
    copies[1].wait()
    quarter = lanes((512, 128)) // 32
    sent = []
    for at in (32, 0):
        value = jnp.zeros((512, 128), F32)
        for ex in range(EXL):
            part = field[:, ex // 2 * 128 : ex // 2 * 128 + 128]
            moved = roll(part, 32 * ex - (ex % 2 * 64 + at))
            value = jnp.where(quarter == ex, moved, value)
        sent.append(value)
    even = parity[0] == 0
    near[...] = jnp.where(even, sent[0], sent[1])
    far[...] = jnp.where(even, sent[1], sent[0])


def widen_kernel(parity, field, got_near, got_far, wide_far, near, far, wide, sems):
    lane = lanes((512, 128))
    even = parity[0] == 0
    before = jnp.where(even, got_far[...], got_near[...])
    after = jnp.where(even, got_near[...], got_far[...])
    copies = []
    for ex in range(EXL):
        own = roll(field[:, ex // 2 * 128 : ex // 2 * 128 + 128], 32 - ex % 2 * 64)
        value = jnp.where(lane < 32, roll(before, -32 * ex), own)
        value = jnp.where(lane < 96, value, roll(after, 96 - 32 * ex))
        part = pl.ds(ex * 512, 512)
        wide[part, :] = value
        copies.append(pltpu.make_async_copy(wide.at[part], wide_far.at[part], sems.at[ex]))
        copies[ex].start()

    def send(up, down):
        up[0:1024, :] = wide[1024:2048, :]
        up[1024:1088, :] = wide[960:1024, :]
        down[0:1024, :] = wide[0:1024, :]
        down[1024:1088, :] = wide[1024:1088, :]

    pl.when(parity[1] == 0)(lambda: send(near, far))
    pl.when(parity[1] != 0)(lambda: send(far, near))
    for copy in copies:
        copy.wait()


def pair_step(old, new, base, block_high, block_low):
    level = lanes((8, 128)) % 8
    for side in range(2):
        at = pl.multiple_of(base + 512 * side, 512)
        for j in range(8):
            nodes = [old[pl.ds(at + i * 64 + j * 8, 8), :] for i in range(8)]
            for row in range(8):
                value = nodes[row]
                for i in range(8):
                    value = value + float(np.float32(ALONG_X[row, i])) * nodes[i]
                if row == 0:
                    value = value + PEN_IN * old[pl.ds(at - 64 + j * 8, 8), :]
                if row == 7:
                    value = value + PEN * old[pl.ds(at + 512 + j * 8, 8), :]
                if j == 0:
                    upper = old[pl.ds(at + row * 64 + 56, 8), :]
                    value = value + PEN * jnp.where(level > 0, roll(upper, 1), nodes[row])
                if j == 7:
                    lower = old[pl.ds(at + row * 64, 8), :]
                    value = value + PEN * jnp.where(level < 7, roll(lower, 127), 0.0)
                new[pl.ds(at + row * 64 + j * 8, 8), :] = value
    for half in range(2):
        left = pl.ds(pl.multiple_of(base + 256 * half, 256), 256)
        right = pl.ds(pl.multiple_of(base + 512 + 256 * half, 256), 256)
        high, low = two(jnp.concatenate([old[left, :], old[right, :]], axis=1))
        value = dot(block_high[...], high) + (
            dot(block_high[...], low) + dot(block_low[...], high)
        )
        new[left, :] = new[left, :] + value[:, 0:128]
        new[right, :] = new[right, :] + value[:, 128:256]
    for side in range(2):
        for i in range(8):
            first = pl.ds(base + 512 * side + i * 64, 8, stride=8)
            last = pl.ds(base + 512 * side + i * 64 + 7, 8, stride=8)
            new[first, :] = new[first, :] + PEN * roll(old[last, :], 8)
            new[last, :] = new[last, :] + PEN * roll(old[first, :], 120)


def gather_features(wall):
    quarter = lanes((64, 128)) // 32
    sides = []
    for side in range(2):
        part = wall[pl.ds(4 * side, 64, stride=8), :]
        for n in range(1, 4):
            part = jnp.where(quarter == n, wall[pl.ds(4 * side + n, 64, stride=8), :], part)
        sides.append(part)
    return jnp.concatenate(sides, axis=1)


def run_pairs(old, new, first, pairs, block_high, block_low):
    def body(p, carry):
        pair_step(old, new, pl.multiple_of((first + 2 * p) * 512, 512), block_high, block_low)
        return carry

    lax.fori_loop(0, pairs, body, 0)
    beyond = (first + 2 * pairs) * 512
    new[first * 512 - 64 : first * 512, :] = jnp.zeros((64, 128), F32)
    new[beyond : beyond + 64, :] = jnp.zeros((64, 128), F32)


def first_step_kernel(
    parity, wide, got_near, got_far, block_high, block_low, new, features_x, features_z, old, wall
):
    def place(left, right):
        old[448:512, :] = left[1024:1088, :]
        old[512:1536, :] = left[0:1024, :]
        old[3584:4608, :] = right[0:1024, :]
        old[4608:4672, :] = right[1024:1088, :]

    pl.when(parity[1] == 0)(lambda: place(got_far, got_near))
    pl.when(parity[1] != 0)(lambda: place(got_near, got_far))
    old[1536:3584, :] = wide[...]

    source = lax.broadcasted_iota(jnp.int32, (256, 128), 0)
    goal = lanes((256, 128)) % 32
    ez = source // 8 % 16
    for out_ref, pairs in ((features_x, (0, 3)), (features_z, (0, 1, 2, 3))):
        total = jnp.zeros((512, 128), F32)
        for n, pair in enumerate(pairs):
            if out_ref is features_x:
                here = (ez >= 4) & (ez < 12)
                slot = (2 * n + source // 128) * 8 + ez - 4
            else:
                here = (ez == 2) | (ez == 3) | (ez == 12) | (ez == 13)
                slot = (2 * n + source // 128) * 4 + jnp.where(ez < 8, ez - 2, ez - 10)
            pick = (here & (source % 8 == 0) & (slot == goal)).astype(BF)
            at = 512 + 1024 * pair
            columns = jnp.concatenate([old[at : at + 512, :], old[at + 512 : at + 1024, :]], axis=1)
            total += dot(columns.astype(BF), pick)
        wall[...] = total
        out_ref[...] = gather_features(wall).astype(BF)
    run_pairs(old, new, 1, 4, block_high, block_low)


def middle_step_kernel(first, pairs):
    def kernel(old, block_high, block_low, new):
        run_pairs(old, new, first, pairs, block_high, block_low)

    return kernel


def last_step_kernel(old, block_high, block_low, out, new):
    run_pairs(old, new, 3, 2, block_high, block_low)
    lane = lanes((512, 128))
    for side in range(2):
        at = (3 + 2 * side) * 512
        out[:, 128 * side : 128 * side + 128] = jnp.where(
            lane < 64,
            roll(new[at : at + 512, :], -32),
            roll(new[at + 512 : at + 1024, :], 32),
        )


def weight_columns(first, second):
    stacked = jnp.concatenate(
        [first, jnp.broadcast_to(second, (8, HID)), jnp.zeros((112, HID), F32)], axis=0
    )
    return jnp.transpose(stacked)


def network_sum(columns, spread, chunk, keep_mask):
    weights = columns.astype(BF)
    parts = []
    lane = lanes((8, 128))
    row = rows((8, 128))
    for i in range(8):
        inputs = jnp.concatenate([chunk(i), jnp.zeros((120, 256), BF)], axis=0)
        before = dot(weights, inputs)
        if keep_mask is not None:
            keep_mask[i] = jnp.where(before > 0.0, 1.0, 0.0).astype(BF)
        active = jnp.maximum(before, 0.0)
        scale = spread[...]
        total = jnp.concatenate(
            [
                jnp.sum(active[:, 0:128] * scale, axis=0, keepdims=True),
                jnp.sum(active[:, 128:256] * scale, axis=0, keepdims=True),
            ],
            axis=1,
        )
        total = jnp.broadcast_to(total, (8, 256))
        piece = jnp.where(lane // 32 == row, total[:, 0:128], 0.0) + jnp.where(
            lane // 32 + 4 == row, total[:, 128:256], 0.0
        )
        piece = piece + roll(piece, 64)
        parts.append(piece + roll(piece, 32))
    return jnp.concatenate(parts, axis=0)


def face_tables(edges):
    node = lax.broadcasted_iota(jnp.int32, (64, 256), 0)
    source = (node == edges[0:1, :]).astype(BF)
    target = (node == edges[1:2, :]).astype(BF)
    forward = (0.25 * dot_t(source, target)).astype(BF)
    backward = (0.25 * dot_t(target, source)).astype(BF)
    return forward, backward


def grad_kernel(
    field, first, second, edges, route, samples, counts,
    total_grad, features, wall, mask, spread, feat,
):
    element = lax.broadcasted_iota(jnp.int32, (256, 128), 0)
    pick = (element == 8 * (lanes((256, 128)) % 32)).astype(BF)
    wall[...] = dot(field[...].astype(BF), pick)
    feat[...] = gather_features(wall)
    features[...] = feat[...].astype(BF)
    slopes = []
    for i in range(8):
        slope = float(np.float32(DERIV[0, 0])) * field[i * 64 : i * 64 + 8, :]
        for j in range(1, 8):
            slope += float(np.float32(DERIV[0, j])) * field[i * 64 + 8 * j : i * 64 + 8 * j + 8, :]
        slopes.append(slope)
    a, b, c = three(jnp.concatenate(slopes, axis=0))
    slope = dot(a, pick) + dot(b, pick) + dot(c, pick)
    target = (STRESS_SCALE * slope).astype(BF).astype(F32)

    columns = weight_columns(first[...].astype(F32), second[...].astype(F32))
    spread[...] = jnp.broadcast_to(columns[:, 8:9], (HID, 128))
    sums = network_sum(
        columns, spread, lambda i: feat[i * 8 : i * 8 + 8, :].astype(BF), mask
    )
    forward, backward = face_tables(edges[...])
    error = sums + exact_dot(backward, sums) - target
    error = error + exact_dot(forward, error)

    learner = lax.broadcasted_iota(jnp.int32, (128, 64), 0)
    hits = (learner == route[...]).astype(BF)
    total = jnp.broadcast_to(jnp.sum(counts[...], axis=0, keepdims=True), (8, 128))
    inverse = 1.0 / (jnp.maximum(total, 1.0) * 256.0)
    a, b, c = three(inverse)
    share = dot(a, hits) + dot(b, hits) + dot(c, hits)
    place = lax.broadcasted_iota(jnp.int32, (128, 64), 0) % 32
    taken = (place == samples[...]).astype(BF)
    a, b, c = three(share)
    total = dot_t(a, taken) + dot_t(b, taken) + dot_t(c, taken)
    error = error * total[0:1, :]

    lane = lanes((8, 128))
    row = rows((8, 128))
    result = jnp.zeros((16, HID), F32)
    for i in range(8):
        own = error[i * 8 : i * 8 + 8, :]
        line = jnp.concatenate(
            [
                jnp.sum(jnp.where(lane // 32 == row, own, 0.0), axis=0, keepdims=True),
                jnp.sum(jnp.where(lane // 32 + 4 == row, own, 0.0), axis=0, keepdims=True),
            ],
            axis=1,
        )
        high, low = two(feat[i * 8 : i * 8 + 8, :] * line)
        result += dot_t(jnp.concatenate([high, low], axis=0), mask[i])
    total_grad[...] = result[0:8] + result[8:16]


def finish_kernel(
    first, second, edges, features_own, features_x, features_z, grad,
    u, columns_y, plane_high, plane_low,
    new_first, new_second, out, spread, state, grown,
):
    table = grad[...]
    weight = first[...].astype(F32)
    output = second[...].astype(F32)
    updated = (weight - LEARN_RATE * (output * table)).astype(BF)
    updated_second = (
        output - LEARN_RATE * jnp.sum(weight * table, axis=0, keepdims=True)
    ).astype(BF)
    new_first[...] = updated
    new_second[...] = updated_second
    columns = weight_columns(updated.astype(F32), updated_second.astype(F32))
    spread[...] = jnp.broadcast_to(columns[:, 8:9], (HID, 128))
    _, backward = face_tables(edges[...])
    lane = lanes((64, 128))
    column, ez = lane // 16, lane % 16
    extended = jnp.zeros((64, 128), F32)
    for features, places in (
        (features_own, (2, 3, 4, 5)),
        (features_x, (0, 1, 6, 7)),
        (features_z, tuple(range(8))),
    ):
        known = features[...].astype(F32)
        sums = network_sum(
            columns, spread, lambda i: known[i * 8 : i * 8 + 8, :].astype(BF), None
        )
        stress = sums + exact_dot(backward, sums)
        for n, place in enumerate(places):
            if features is features_z:
                for low, near in ((2, 2), (12, 10)):
                    inside = (column == place) & (ez >= low) & (ez < low + 2)
                    extended = jnp.where(
                        inside, roll(stress, place * 16 + near - 4 * n), extended
                    )
            else:
                inside = (column == place) & (ez >= 4) & (ez < 12)
                extended = jnp.where(inside, roll(stress, place * 16 + 4 - 8 * n), extended)

    current = extended
    source = lax.broadcasted_iota(jnp.int32, (128, 256), 0)
    element = lanes((128, 256))
    centre = (source == (2 + element // 64) * 16 + 4 + (element // 8) % 8).astype(BF)
    for p in range(FLOW_STEPS):
        high, low = two(current)
        grown[p] = dot(high, centre) + dot(low, centre)
        if p == FLOW_STEPS - 1:
            break
        state[...] = current
        first_z, last_z = state[pl.ds(0, 8, stride=8), :], state[pl.ds(7, 8, stride=8), :]
        state[...] = dot(plane_high[...], high) + (
            dot(plane_high[...], low) + dot(plane_low[...], high)
        )
        at = pl.ds(0, 8, stride=8)
        state[at, :] = state[at, :] + PEN * roll(last_z, 1)
        at = pl.ds(7, 8, stride=8)
        state[at, :] = state[at, :] + PEN * roll(first_z, 127)
        moved = state[...]
        current = jnp.concatenate(
            [
                moved[0:8] + PEN_IN * roll(current[56:64], 16),
                moved[8:56],
                moved[56:64] + PEN * roll(current[0:8], 112),
            ],
            axis=0,
        )
    for i in range(8):
        for j in range(8):
            at = i * 64 + j * 8
            value = u[at : at + 8, :]
            for p in range(FLOW_STEPS):
                value += columns_y[p * 8 + j : p * 8 + j + 1, :] * grown[p, i * 8 : i * 8 + 8, :]
            out[at : at + 8, :] = value


VM = pl.BlockSpec(memory_space=pltpu.VMEM)
SM = pl.BlockSpec(memory_space=pltpu.SMEM)
HB = pl.BlockSpec(memory_space=pltpu.HBM)


def sds(shape, dtype=F32):
    return jax.ShapeDtypeStruct(shape, dtype)


def call(kernel, out_shape, scratch, scalars, *args, arrays=VM, results=None, limit=24 << 10):
    return pl.pallas_call(
        kernel,
        out_shape=out_shape,
        in_specs=[SM] * scalars + [arrays] * (len(args) - scalars),
        out_specs=results or jax.tree.map(lambda _: VM, out_shape),
        scratch_shapes=scratch,
        compiler_params=pltpu.CompilerParams(vmem_limit_bytes=limit << 10),
        cost_estimate=pl.CostEstimate(flops=4 * 10**9, transcendentals=0, bytes_accessed=10**6),
    )(*args)


def shards(field, first_weight, second_weight, face_edges, sample_index, route):
    both = ("solver", "group")
    learners, groups = lax.axis_size("solver"), lax.axis_size("group")
    devices = learners * groups

    def partners(value, shift):
        return [
            lax.ppermute(value, both, [(d, d ^ (m << shift)) for d in range(devices)])
            for m in (1, 2, 3)
        ]

    def swapped(near, far, axis):
        size = lax.axis_size(axis)
        pairs = [(i, i ^ 1) for i in range(size)]
        others = [(i, (i - 1 if i % 2 == 0 else i + 1) % size) for i in range(size)]
        return lax.ppermute(near, axis, pairs), lax.ppermute(far, axis, others)

    field = field.reshape(512, 256)
    second_row = second_weight.reshape(1, HID)
    route_row = route.reshape(1, 64)
    sample_row = sample_index.reshape(1, 64)
    solver, group = lax.axis_index("solver"), lax.axis_index("group")
    parity = jnp.stack([group & 1, solver & 1]).astype(jnp.int32)
    block_high, block_low = jnp.asarray(VOLUME_HIGH), jnp.asarray(VOLUME_LOW)

    counts, near, far = call(
        start_kernel,
        [sds((64, 128)), sds((512, 128)), sds((512, 128))],
        [
            pltpu.VMEM((512, 256), F32),
            pltpu.VMEM((1, 64), jnp.int32),
            pltpu.SemaphoreType.DMA((2,)),
        ],
        1,
        parity, field, route_row,
        arrays=HB,
        limit=54500,
    )
    near, far = swapped(near, far, "group")
    counts = lax.all_to_all(counts, "solver", 0, 0, tiled=True)
    wide, near, far = call(
        widen_kernel,
        [sds((2048, 128)), sds((1088, 128)), sds((1088, 128))],
        [pltpu.VMEM((2048, 128), F32), pltpu.SemaphoreType.DMA((4,))],
        1,
        parity, field, near, far,
        results=[HB, VM, VM],
        limit=52500,
    )
    near, far = swapped(near, far, "solver")

    grad, features = call(
        grad_kernel,
        [sds((8, HID)), sds((64, 256), BF)],
        [
            pltpu.VMEM((512, 128), F32),
            pltpu.VMEM((8, HID, 256), BF),
            pltpu.VMEM((HID, 128), F32),
            pltpu.VMEM((64, 256), F32),
        ],
        0,
        field, first_weight, second_row, face_edges, route_row, sample_row, counts,
    )

    state = sds((5120, 128))
    space = pltpu.VMEM((5120, 128), F32)

    def middle(u, first, pairs):
        return call(
            middle_step_kernel(first, pairs), state, [], 0,
            u, block_high, block_low,
        )

    for number, shift in enumerate((6, 2, 4, 0)):
        got = partners(grad, shift)
        if number == 1:
            u, features_x, features_z = call(
                first_step_kernel,
                [state, sds((64, 256), BF), sds((64, 256), BF)],
                [space, pltpu.VMEM((512, 128), F32)],
                1,
                parity, wide, near, far, block_high, block_low,
            )
        if number == 2:
            u = middle(middle(u, 1, 4), 2, 3)
        if number == 3:
            u = call(
                last_step_kernel, sds((512, 256)), [space], 0,
                middle(u, 2, 3), block_high, block_low,
            )
        grad = (grad + got[0]) + (got[1] + got[2])
    new_first, new_second, new_field = call(
        finish_kernel,
        [sds((8, HID), BF), sds((1, HID), BF), sds((512, 256))],
        [
            pltpu.VMEM((HID, 128), F32),
            pltpu.VMEM((64, 128), F32),
            pltpu.VMEM((FLOW_STEPS, 64, 256), F32),
        ],
        0,
        first_weight, second_row, face_edges, features, features_x, features_z,
        grad, u, jnp.asarray(COLUMNS, F32), jnp.asarray(PLANE_HIGH), jnp.asarray(PLANE_LOW),
    )
    return (new_field.reshape(8, 8, 8, 256), new_first, new_second.reshape(HID, 1))


def solution(mesh):
    return jax.shard_map(
        shards,
        mesh=mesh,
        in_specs=(
            P(None, None, None, ("solver", "group")),
            P(),
            P(),
            P(),
            P(("solver", "group")),
            P(("solver", "group"), None),
        ),
        out_specs=(P(None, None, None, ("solver", "group")), P(), P()),
        check_vma=False,
    )
```

profile of v0, /device:TPU:2, one launch (start us, length us, event | category | flops | bytes accessed | tf_op | source)
XLA Modules:
  0.0 77.3 jit_solution(15791129495356675282)
XLA Ops:
  1.4 2.2 %shard_map.130 = (f32[64,128]{1,0:T(8,128)}, f32[512,128]{1,0:T(8,128)S(1)}, f32[512,128]{1,0:T(8,128)S(1)}) custom-call(s32[2]{0:T(128)S(1)} %pad_add_fusion.parity, f32[512,256]{1,0:T(8,128)} %bitcast.13, s32[1,64]{1,0:T(1,128)S(1)} %bitcast.18), custom_call_target="tpu_custom_call" | custom-call | flops 4000000000 | bytes 1000000 | tf_op jit(solution)/shard_map/pallas_call | solution.py:503
  3.6 9.4 %all-to-all-start = ((f32[64,1,128]{2,1,0:T(1,128)}), f32[64,1,128]{2,1,0:T(1,128)S(1)}, u32[]{:S(2)}, u32[]{:S(2)}) async-start(f32[64,1,128]{2,1,0:T(1,128)} %bitcast.7), calls=%async_computation | async-start | bytes 65536 | tf_op jit(solution)/shard_map/all_to_all | solution.py:553
  13.0 3.4 %collective-permute-start = (f32[512,128]{1,0:T(8,128)S(1)}, f32[512,128]{1,0:T(8,128)S(1)}, u32[]{:S(2)}, u32[]{:S(2)}) collective-permute-start(f32[512,128]{1,0:T(8,128)S(1)} %get-tuple-element.19), channel_id=1, source_target_pairs={{0,1},{1,0},{2,3},{3,2},{4,5},{5,4},{6,7},{7,6},{8,9},{9,8},{10,11... | collective-permute-start | bytes 786440 | tf_op jit(solution)/shard_map/ppermute | solution.py:529
  16.4 3.6 %collective-permute-start.1 = (f32[512,128]{1,0:T(8,128)S(1)}, f32[512,128]{1,0:T(8,128)S(1)}, u32[]{:S(2)}, u32[]{:S(2)}) collective-permute-start(f32[512,128]{1,0:T(8,128)S(1)} %get-tuple-element.20), channel_id=1, source_target_pairs={{0,3},{1,2},{2,1},{3,0},{4,7},{5,6},{6,5},{7,4},{8,11},{9,10},{10,... | collective-permute-start | bytes 786440 | tf_op jit(solution)/shard_map/ppermute | solution.py:529
  20.1 3.5 %shard_map.131 = (f32[8,1024]{1,0:T(8,128)S(1)}, bf16[64,256]{1,0:T(8,128)(2,1)S(1)}) custom-call(f32[512,256]{1,0:T(8,128)S(1)} %bitcast.14, bf16[8,1024]{1,0:T(8,128)(2,1)S(1)} %copy-done.1, bf16[1,1024]{1,0:T(2,128)(2,1)S(1)} %bitcast.16, s32[2,256]{1,0:T(2,128)S(1)} %copy-done.3, s32[1,64]{1,0:T(1,128)S(1)} %bitcast.19, s32[1,64]{1,0:T(1,128)S(1)} %bitcast.20, ...), custom_call_target="tpu_custom_call" | custom-call | flops 4000000000 | bytes 1000000 | tf_op jit(solution)/shard_map/pallas_call | solution.py:503
  23.6 2.9 %collective-permute-start.6 = (f32[8,1024]{1,0:T(8,128)S(1)}, f32[8,1024]{1,0:T(8,128)S(1)}, u32[]{:S(2)}, u32[]{:S(2)}) collective-permute-start(f32[8,1024]{1,0:T(8,128)S(1)} %get-tuple-element.26), channel_id=1, source_target_pairs={{0,192},{1,193},{2,194},{3,195},{4,196},{5,197},{6,198},{7,199},{8... | collective-permute-start | bytes 98312 | tf_op jit(solution)/shard_map/ppermute | solution.py:521
  28.7 3.1 %collective-permute-done.5 = f32[8,1024]{1,0:T(8,128)S(1)} collective-permute-done((f32[8,1024]{1,0:T(8,128)S(1)}, f32[8,1024]{1,0:T(8,128)S(1)}, u32[]{:S(2)}, u32[]{:S(2)}) %collective-permute-start.5) | collective-permute-done | bytes 32800 | tf_op jit(solution)/shard_map/ppermute | solution.py:521
  32.0 1.6 %collective-permute-start.8 = (f32[8,1024]{1,0:T(8,128)S(1)}, f32[8,1024]{1,0:T(8,128)S(1)}, u32[]{:S(2)}, u32[]{:S(2)}) collective-permute-start(f32[8,1024]{1,0:T(8,128)S(1)} %add_add_fusion.3), channel_id=1, source_target_pairs={{0,8},{1,9},{2,10},{3,11},{4,12},{5,13},{6,14},{7,15},{8,0},{9,1},... | collective-permute-start | bytes 98312 | tf_op jit(solution)/shard_map/ppermute | solution.py:521
  33.9 2.0 %shard_map.132 = (f32[2048,128]{1,0:T(8,128)}, f32[1088,128]{1,0:T(8,128)S(1)}, f32[1088,128]{1,0:T(8,128)S(1)}) custom-call(s32[2]{0:T(128)S(1)} %pad_add_fusion.parity, f32[512,256]{1,0:T(8,128)S(1)} %bitcast.15, f32[512,128]{1,0:T(8,128)S(1)} %collective-permute-done.got_near, f32[512,128]{1,0:T(8,128)S(1)} %collective-permute-done.1.got_far), custom_call_target="tpu_custom_call" | custom-call | flops 4000000000 | bytes 1000000 | tf_op jit(solution)/shard_map/pallas_call | solution.py:503
  36.2 1.3 %collective-permute-start.3 = (f32[1088,128]{1,0:T(8,128)S(1)}, f32[1088,128]{1,0:T(8,128)S(1)}, u32[]{:S(2)}, u32[]{:S(2)}) collective-permute-start(f32[1088,128]{1,0:T(8,128)S(1)} %get-tuple-element.23), channel_id=1, source_target_pairs={{0,252},{4,8},{8,4},{12,16},{16,12},{20,24},{24,20},{28,32},{32,28... | collective-permute-start | bytes 1671176 | tf_op jit(solution)/shard_map/ppermute | solution.py:529
  37.6 1.6 %collective-permute-start.12 = (f32[8,1024]{1,0:T(8,128)S(1)}, f32[8,1024]{1,0:T(8,128)S(1)}, u32[]{:S(2)}, u32[]{:S(2)}) collective-permute-start(f32[8,1024]{1,0:T(8,128)S(1)} %add_add_fusion.2), channel_id=1, source_target_pairs={{0,48},{1,49},{2,50},{3,51},{4,52},{5,53},{6,54},{7,55},{8,56},{9,... | collective-permute-start | bytes 98312 | tf_op jit(solution)/shard_map/ppermute | solution.py:521
  39.2 4.1 %collective-permute-start.11 = (f32[8,1024]{1,0:T(8,128)S(1)}, f32[8,1024]{1,0:T(8,128)S(1)}, u32[]{:S(2)}, u32[]{:S(2)}) collective-permute-start(f32[8,1024]{1,0:T(8,128)S(1)} %add_add_fusion.2), channel_id=1, source_target_pairs={{0,32},{1,33},{2,34},{3,35},{4,36},{5,37},{6,38},{7,39},{8,40},{9,... | collective-permute-start | bytes 98312 | tf_op jit(solution)/shard_map/ppermute | solution.py:521
  43.3 1.9 %collective-permute-done.11 = f32[8,1024]{1,0:T(8,128)S(1)} collective-permute-done((f32[8,1024]{1,0:T(8,128)S(1)}, f32[8,1024]{1,0:T(8,128)S(1)}, u32[]{:S(2)}, u32[]{:S(2)}) %collective-permute-start.11) | collective-permute-done | bytes 32800 | tf_op jit(solution)/shard_map/ppermute | solution.py:521
  45.1 2.4 %collective-permute-done.10 = f32[8,1024]{1,0:T(8,128)S(1)} collective-permute-done((f32[8,1024]{1,0:T(8,128)S(1)}, f32[8,1024]{1,0:T(8,128)S(1)}, u32[]{:S(2)}, u32[]{:S(2)}) %collective-permute-start.10) | collective-permute-done | bytes 32800 | tf_op jit(solution)/shard_map/ppermute | solution.py:521
  47.5 3.2 %collective-permute-start.15 = (f32[8,1024]{1,0:T(8,128)S(1)}, f32[8,1024]{1,0:T(8,128)S(1)}, u32[]{:S(2)}, u32[]{:S(2)}) collective-permute-start(f32[8,1024]{1,0:T(8,128)S(1)} %add_add_fusion.1), channel_id=1, source_target_pairs={{0,3},{1,2},{2,1},{3,0},{4,7},{5,6},{6,5},{7,4},{8,11},{9,10},{10,... | collective-permute-start | bytes 98312 | tf_op jit(solution)/shard_map/ppermute | solution.py:521
  50.8 2.1 %collective-permute-start.14 = (f32[8,1024]{1,0:T(8,128)S(1)}, f32[8,1024]{1,0:T(8,128)S(1)}, u32[]{:S(2)}, u32[]{:S(2)}) collective-permute-start(f32[8,1024]{1,0:T(8,128)S(1)} %add_add_fusion.1), channel_id=1, source_target_pairs={{0,2},{1,3},{2,0},{3,1},{4,6},{5,7},{6,4},{7,5},{8,10},{9,11},{10,... | collective-permute-start | bytes 98312 | tf_op jit(solution)/shard_map/ppermute | solution.py:521
  52.8 1.5 %collective-permute-start.13 = (f32[8,1024]{1,0:T(8,128)S(1)}, f32[8,1024]{1,0:T(8,128)S(1)}, u32[]{:S(2)}, u32[]{:S(2)}) collective-permute-start(f32[8,1024]{1,0:T(8,128)S(1)} %add_add_fusion.1), channel_id=1, source_target_pairs={{0,1},{1,0},{2,3},{3,2},{4,5},{5,4},{6,7},{7,6},{8,9},{9,8},{10,11... | collective-permute-start | bytes 98312 | tf_op jit(solution)/shard_map/ppermute | solution.py:521
  54.8 3.8 %collective-permute-done.14 = f32[8,1024]{1,0:T(8,128)S(1)} collective-permute-done((f32[8,1024]{1,0:T(8,128)S(1)}, f32[8,1024]{1,0:T(8,128)S(1)}, u32[]{:S(2)}, u32[]{:S(2)}) %collective-permute-start.14) | collective-permute-done | bytes 32800 | tf_op jit(solution)/shard_map/ppermute | solution.py:521
  59.9 3.6 %shard_map.133 = (f32[5120,128]{1,0:T(8,128)S(1)}, bf16[64,256]{1,0:T(8,128)(2,1)S(1)}, bf16[64,256]{1,0:T(8,128)(2,1)S(1)}) custom-call(s32[2]{0:T(128)S(1)} %pad_add_fusion.parity, f32[2048,128]{1,0:T(8,128)S(1)} %copy-done.12, f32[1088,128]{1,0:T(8,128)S(1)} %collective-permute-done.2.got_near, f32[1088,128]{1,0:T(8,128)S(1)} %collective-permute-done.3.got_far, ...), custom_call_target="tpu_custom_call" | custom-call | flops 4000000000 | bytes 1000000 | tf_op jit(solution)/shard_map/pallas_call | solution.py:503
  63.5 2.3 %shard_map.134.old = f32[5120,128]{1,0:T(8,128)S(1)} custom-call(f32[5120,128]{1,0:T(8,128)S(1)} %get-tuple-element.27.old, bf16[256,256]{1,0:T(8,128)(2,1)S(1)} %copy-done.8, bf16[256,256]{1,0:T(8,128)(2,1)S(1)} %copy-done.7), custom_call_target="tpu_custom_call" | custom-call | flops 4000000000 | bytes 1000000 | tf_op jit(solution)/shard_map/pallas_call | solution.py:503
  65.8 1.8 %shard_map.135.old = f32[5120,128]{1,0:T(8,128)S(1)} custom-call(f32[5120,128]{1,0:T(8,128)S(1)} %shard_map.134.old, bf16[256,256]{1,0:T(8,128)(2,1)S(1)} %copy-done.8, bf16[256,256]{1,0:T(8,128)(2,1)S(1)} %copy-done.7), custom_call_target="tpu_custom_call" | custom-call | flops 4000000000 | bytes 1000000 | tf_op jit(solution)/shard_map/pallas_call | solution.py:503
  67.6 1.8 %shard_map.136.old = f32[5120,128]{1,0:T(8,128)S(1)} custom-call(f32[5120,128]{1,0:T(8,128)S(1)} %shard_map.135.old, bf16[256,256]{1,0:T(8,128)(2,1)S(1)} %copy-done.8, bf16[256,256]{1,0:T(8,128)(2,1)S(1)} %copy-done.7), custom_call_target="tpu_custom_call" | custom-call | flops 4000000000 | bytes 1000000 | tf_op jit(solution)/shard_map/pallas_call | solution.py:503
  69.4 1.5 %shard_map.137.u = f32[512,256]{1,0:T(8,128)S(1)} custom-call(f32[5120,128]{1,0:T(8,128)S(1)} %shard_map.136.old, bf16[256,256]{1,0:T(8,128)(2,1)S(1)} %copy-done.8, bf16[256,256]{1,0:T(8,128)(2,1)S(1)} %copy-done.7), custom_call_target="tpu_custom_call" | custom-call | flops 4000000000 | bytes 1000000 | tf_op jit(solution)/shard_map/pallas_call | solution.py:503
  70.9 6.4 %shard_map.138 = (bf16[8,1024]{1,0:T(8,128)(2,1)}, bf16[1,1024]{1,0:T(2,128)(2,1)}, f32[512,256]{1,0:T(8,128)}) custom-call(bf16[8,1024]{1,0:T(8,128)(2,1)S(1)} %copy-done.1, bf16[1,1024]{1,0:T(2,128)(2,1)S(1)} %bitcast.17, s32[2,256]{1,0:T(2,128)S(1)} %copy-done.3, bf16[64,256]{1,0:T(8,128)(2,1)S(1)} %get-tuple-element.18.features_own, ...), custom_call_target="tpu_custom_call" | custom-call | flops 4000000000 | bytes 1000000 | tf_op jit(solution)/shard_map/pallas_call | solution.py:503
  (50 shorter events, 5.6 us)
Async XLA Ops:
  1.4 18.7 %copy-start.1 = (bf16[8,1024]{1,0:T(8,128)(2,1)S(1)}, bf16[8,1024]{1,0:T(8,128)(2,1)}, u32[]{:S(2)}) copy-start(bf16[8,1024]{1,0:T(8,128)(2,1)} %first.3) | copy-start | bytes 49156
  1.4 18.7 %copy-start.2 = (bf16[1024,1]{0,1:T(2,128)(2,1)S(1)}, bf16[1024,1]{0,1:T(2,128)(2,1)}, u32[]{:S(2)}) copy-start(bf16[1024,1]{0,1:T(2,128)(2,1)} %param.13) | copy-start | bytes 6148
  1.4 18.7 %copy-start.3 = (s32[2,256]{1,0:T(2,128)S(1)}, s32[2,256]{1,0:T(2,128)}, u32[]{:S(2)}) copy-start(s32[2,256]{1,0:T(2,128)} %edges.3) | copy-start | bytes 6148
  1.4 18.7 %copy-start.5 = (s32[64,1]{0,1:T(1,128)S(1)}, s32[64,1]{0,1:T(1,128)}, u32[]{:S(2)}) copy-start(s32[64,1]{0,1:T(1,128)} %param.16) | copy-start | bytes 772
  1.4 18.7 %copy-start.6 = (s32[64]{0:T(128)S(1)}, s32[64]{0:T(128)}, u32[]{:S(2)}) copy-start(s32[64]{0:T(128)} %param.15) | copy-start | bytes 772
  3.6 16.4 %all-to-all-start = ((f32[64,1,128]{2,1,0:T(1,128)}), f32[64,1,128]{2,1,0:T(1,128)S(1)}, u32[]{:S(2)}, u32[]{:S(2)}) async-start(f32[64,1,128]{2,1,0:T(1,128)} %bitcast.7), calls=%async_computation | async-start | bytes 65536 | tf_op jit(solution)/shard_map/all_to_all | solution.py:553
  13.0 20.8 %collective-permute-start = (f32[512,128]{1,0:T(8,128)S(1)}, f32[512,128]{1,0:T(8,128)S(1)}, u32[]{:S(2)}, u32[]{:S(2)}) collective-permute-start(f32[512,128]{1,0:T(8,128)S(1)} %get-tuple-element.19), channel_id=1, source_target_pairs={{0,1},{1,0},{2,3},{3,2},{4,5},{5,4},{6,7},{7,6},{8,9},{9,8},{10,11... | collective-permute-start | bytes 786440 | tf_op jit(solution)/shard_map/ppermute | solution.py:529
  16.4 17.5 %collective-permute-start.1 = (f32[512,128]{1,0:T(8,128)S(1)}, f32[512,128]{1,0:T(8,128)S(1)}, u32[]{:S(2)}, u32[]{:S(2)}) collective-permute-start(f32[512,128]{1,0:T(8,128)S(1)} %get-tuple-element.20), channel_id=1, source_target_pairs={{0,3},{1,2},{2,1},{3,0},{4,7},{5,6},{6,5},{7,4},{8,11},{9,10},{10,... | collective-permute-start | bytes 786440 | tf_op jit(solution)/shard_map/ppermute | solution.py:529
  23.6 5.1 %collective-permute-start.6 = (f32[8,1024]{1,0:T(8,128)S(1)}, f32[8,1024]{1,0:T(8,128)S(1)}, u32[]{:S(2)}, u32[]{:S(2)}) collective-permute-start(f32[8,1024]{1,0:T(8,128)S(1)} %get-tuple-element.26), channel_id=1, source_target_pairs={{0,192},{1,193},{2,194},{3,195},{4,196},{5,197},{6,198},{7,199},{8... | collective-permute-start | bytes 98312 | tf_op jit(solution)/shard_map/ppermute | solution.py:521
  26.5 5.4 %collective-permute-start.5 = (f32[8,1024]{1,0:T(8,128)S(1)}, f32[8,1024]{1,0:T(8,128)S(1)}, u32[]{:S(2)}, u32[]{:S(2)}) collective-permute-start(f32[8,1024]{1,0:T(8,128)S(1)} %get-tuple-element.26), channel_id=1, source_target_pairs={{0,128},{1,129},{2,130},{3,131},{4,132},{5,133},{6,134},{7,135},{8... | collective-permute-start | bytes 98312 | tf_op jit(solution)/shard_map/ppermute | solution.py:521
  27.1 4.8 %collective-permute-start.4 = (f32[8,1024]{1,0:T(8,128)S(1)}, f32[8,1024]{1,0:T(8,128)S(1)}, u32[]{:S(2)}, u32[]{:S(2)}) collective-permute-start(f32[8,1024]{1,0:T(8,128)S(1)} %get-tuple-element.26), channel_id=1, source_target_pairs={{0,64},{1,65},{2,66},{3,67},{4,68},{5,69},{6,70},{7,71},{8,72},{9,... | collective-permute-start | bytes 98312 | tf_op jit(solution)/shard_map/ppermute | solution.py:521
  31.9 26.7 %copy-start.7 = (bf16[256,256]{1,0:T(8,128)(2,1)S(1)}, bf16[256,256]{1,0:T(8,128)(2,1)}, u32[]{:S(2)}) copy-start(bf16[256,256]{1,0:T(8,128)(2,1)} %constant.22.clone.block_low) | copy-start | bytes 393220
  31.9 26.7 %copy-start.8 = (bf16[256,256]{1,0:T(8,128)(2,1)S(1)}, bf16[256,256]{1,0:T(8,128)(2,1)}, u32[]{:S(2)}) copy-start(bf16[256,256]{1,0:T(8,128)(2,1)} %constant.21.clone.block_high) | copy-start | bytes 393220
  31.9 5.7 %collective-permute-start.9 = (f32[8,1024]{1,0:T(8,128)S(1)}, f32[8,1024]{1,0:T(8,128)S(1)}, u32[]{:S(2)}, u32[]{:S(2)}) collective-permute-start(f32[8,1024]{1,0:T(8,128)S(1)} %add_add_fusion.3), channel_id=1, source_target_pairs={{0,12},{1,13},{2,14},{3,15},{4,8},{5,9},{6,10},{7,11},{8,4},{9,5},... | collective-permute-start | bytes 98312 | tf_op jit(solution)/shard_map/ppermute | solution.py:521
  32.0 5.6 %collective-permute-start.8 = (f32[8,1024]{1,0:T(8,128)S(1)}, f32[8,1024]{1,0:T(8,128)S(1)}, u32[]{:S(2)}, u32[]{:S(2)}) collective-permute-start(f32[8,1024]{1,0:T(8,128)S(1)} %add_add_fusion.3), channel_id=1, source_target_pairs={{0,8},{1,9},{2,10},{3,11},{4,12},{5,13},{6,14},{7,15},{8,0},{9,1},... | collective-permute-start | bytes 98312 | tf_op jit(solution)/shard_map/ppermute | solution.py:521
  33.6 4.0 %collective-permute-start.7 = (f32[8,1024]{1,0:T(8,128)S(1)}, f32[8,1024]{1,0:T(8,128)S(1)}, u32[]{:S(2)}, u32[]{:S(2)}) collective-permute-start(f32[8,1024]{1,0:T(8,128)S(1)} %add_add_fusion.3), channel_id=1, source_target_pairs={{0,4},{1,5},{2,6},{3,7},{4,0},{5,1},{6,2},{7,3},{8,12},{9,13},{10,... | collective-permute-start | bytes 98312 | tf_op jit(solution)/shard_map/ppermute | solution.py:521
  35.9 22.7 %collective-permute-start.2 = (f32[1088,128]{1,0:T(8,128)S(1)}, f32[1088,128]{1,0:T(8,128)S(1)}, u32[]{:S(2)}, u32[]{:S(2)}) collective-permute-start(f32[1088,128]{1,0:T(8,128)S(1)} %get-tuple-element.22), channel_id=1, source_target_pairs={{0,4},{4,0},{8,12},{12,8},{16,20},{20,16},{24,28},{28,24},{32,36},... | collective-permute-start | bytes 1671176 | tf_op jit(solution)/shard_map/ppermute | solution.py:529
  36.2 22.4 %collective-permute-start.3 = (f32[1088,128]{1,0:T(8,128)S(1)}, f32[1088,128]{1,0:T(8,128)S(1)}, u32[]{:S(2)}, u32[]{:S(2)}) collective-permute-start(f32[1088,128]{1,0:T(8,128)S(1)} %get-tuple-element.23), channel_id=1, source_target_pairs={{0,252},{4,8},{8,4},{12,16},{16,12},{20,24},{24,20},{28,32},{32,28... | collective-permute-start | bytes 1671176 | tf_op jit(solution)/shard_map/ppermute | solution.py:529
  37.6 5.7 %collective-permute-start.12 = (f32[8,1024]{1,0:T(8,128)S(1)}, f32[8,1024]{1,0:T(8,128)S(1)}, u32[]{:S(2)}, u32[]{:S(2)}) collective-permute-start(f32[8,1024]{1,0:T(8,128)S(1)} %add_add_fusion.2), channel_id=1, source_target_pairs={{0,48},{1,49},{2,50},{3,51},{4,52},{5,53},{6,54},{7,55},{8,56},{9,... | collective-permute-start | bytes 98312 | tf_op jit(solution)/shard_map/ppermute | solution.py:521
  39.2 6.0 %collective-permute-start.11 = (f32[8,1024]{1,0:T(8,128)S(1)}, f32[8,1024]{1,0:T(8,128)S(1)}, u32[]{:S(2)}, u32[]{:S(2)}) collective-permute-start(f32[8,1024]{1,0:T(8,128)S(1)} %add_add_fusion.2), channel_id=1, source_target_pairs={{0,32},{1,33},{2,34},{3,35},{4,36},{5,37},{6,38},{7,39},{8,40},{9,... | collective-permute-start | bytes 98312 | tf_op jit(solution)/shard_map/ppermute | solution.py:521
  43.3 4.3 %collective-permute-start.10 = (f32[8,1024]{1,0:T(8,128)S(1)}, f32[8,1024]{1,0:T(8,128)S(1)}, u32[]{:S(2)}, u32[]{:S(2)}) collective-permute-start(f32[8,1024]{1,0:T(8,128)S(1)} %add_add_fusion.2), channel_id=1, source_target_pairs={{0,16},{1,17},{2,18},{3,19},{4,20},{5,21},{6,22},{7,23},{8,24},{9,... | collective-permute-start | bytes 98312 | tf_op jit(solution)/shard_map/ppermute | solution.py:521
  47.5 7.2 %collective-permute-start.15 = (f32[8,1024]{1,0:T(8,128)S(1)}, f32[8,1024]{1,0:T(8,128)S(1)}, u32[]{:S(2)}, u32[]{:S(2)}) collective-permute-start(f32[8,1024]{1,0:T(8,128)S(1)} %add_add_fusion.1), channel_id=1, source_target_pairs={{0,3},{1,2},{2,1},{3,0},{4,7},{5,6},{6,5},{7,4},{8,11},{9,10},{10,... | collective-permute-start | bytes 98312 | tf_op jit(solution)/shard_map/ppermute | solution.py:521
  50.8 7.8 %collective-permute-start.14 = (f32[8,1024]{1,0:T(8,128)S(1)}, f32[8,1024]{1,0:T(8,128)S(1)}, u32[]{:S(2)}, u32[]{:S(2)}) collective-permute-start(f32[8,1024]{1,0:T(8,128)S(1)} %add_add_fusion.1), channel_id=1, source_target_pairs={{0,2},{1,3},{2,0},{3,1},{4,6},{5,7},{6,4},{7,5},{8,10},{9,11},{10,... | collective-permute-start | bytes 98312 | tf_op jit(solution)/shard_map/ppermute | solution.py:521
  52.8 5.7 %collective-permute-start.13 = (f32[8,1024]{1,0:T(8,128)S(1)}, f32[8,1024]{1,0:T(8,128)S(1)}, u32[]{:S(2)}, u32[]{:S(2)}) collective-permute-start(f32[8,1024]{1,0:T(8,128)S(1)} %add_add_fusion.1), channel_id=1, source_target_pairs={{0,1},{1,0},{2,3},{3,2},{4,5},{5,4},{6,7},{7,6},{8,9},{9,8},{10,11... | collective-permute-start | bytes 98312 | tf_op jit(solution)/shard_map/ppermute | solution.py:521
  (6 other events, 25.2 us)
where the time goes:
time: 77.5 us; the launch traced here: 77.3 us
  starting transfers between devices  36.5 us (47%)
  Pallas kernels  25.1 us (32%)
  waiting for transfers between devices  12.8 us (17%)
  local copies, waits for them, and re-layouts  1.93 us (2%)
  between operations  0.89 us (1%)
    pallas_call x9, Pallas kernels, call(): pl.pallas_call(kernel, out_shape=out_shape, in_specs=[SM] * scalars + [ar...  25.1 us
    ppermute x12, starting transfers between devices, partners(): lax.ppermute(value, both, [(d, d ^ m << shift) for d in range(devices)])  18.5 us
    ppermute x12, waiting for transfers between devices, partners(): lax.ppermute(value, both, [(d, d ^ m << shift) for d in range(devices)])  12.7 us
    all_to_all x1, starting transfers between devices, shards(): counts = lax.all_to_all(counts, 'solver', 0, 0, tiled=True)  9.39 us
    ppermute x4, starting transfers between devices, swapped(): return (lax.ppermute(near, axis, pairs), lax.ppermute(far, axis, others))  8.59 us
    unnamed x26, local copies, waits for them, and re-layouts  1.93 us
  transfers between devices with their start and end apart: 17, of which 7 were waited for; matrix products, arithmetic and copies ran while one was open for 0% of the time, Pallas kernels for 7%

commit v1 on v0

--- a/solution.py
+++ b/solution.py
@@ -147,10 +147,15 @@
 
 
 def start_kernel(parity, field_far, route_far, counts, near, far, field, route, sems):
-    copies = [
-        pltpu.make_async_copy(route_far, route, sems.at[0]),
-        pltpu.make_async_copy(field_far, field, sems.at[1]),
-    ]
+    copies = [pltpu.make_async_copy(route_far, route, sems.at[0])]
+    for half in range(2):
+        copies.append(
+            pltpu.make_async_copy(
+                field_far.at[:, pl.ds(128 * half, 128)],
+                field.at[pl.ds(512 * half, 512), :],
+                sems.at[1 + half],
+            )
+        )
     for copy in copies:
         copy.start()
     copies[0].wait()
@@ -158,34 +163,55 @@
     hits = (learner == route[...]).astype(BF)
     counts[...] = dot_t(jnp.ones((64, 64), BF), hits)
     copies[1].wait()
-    quarter = lanes((512, 128)) // 32
+    copies[2].wait()
+    sixteenth = lanes((512, 128)) // 16
+    eighth = lanes((64, 128)) // 8
+    left = lanes((256, 128)) < 64
     sent = []
-    for at in (32, 0):
+    for at, node, face_at in ((48, 7, 40), (0, 0, 16)):
         value = jnp.zeros((512, 128), F32)
+        face = jnp.zeros((64, 128), F32)
         for ex in range(EXL):
-            part = field[:, ex // 2 * 128 : ex // 2 * 128 + 128]
-            moved = roll(part, 32 * ex - (ex % 2 * 64 + at))
-            value = jnp.where(quarter == ex, moved, value)
-        sent.append(value)
+            start, base = ex // 2 * 512, ex % 2 * 64
+            moved = roll(field[start : start + 512, :], 16 * ex - base - at)
+            value = jnp.where(sixteenth == ex, moved, value)
+            moved = roll(field[pl.ds(start + node, 64, stride=8), :], 8 * ex - base - face_at)
+            face = jnp.where(eighth == ex, moved, face)
+        quarter = lanes((16, 128)) // 32
+        packed = face[0:16]
+        for q in range(1, 4):
+            packed = jnp.where(quarter == q, roll(face[16 * q : 16 * q + 16], 32 * q), packed)
+        sent.append((jnp.where(left, value[0:256], roll(value[256:512], 64)), packed))
     even = parity[0] == 0
-    near[...] = jnp.where(even, sent[0], sent[1])
-    far[...] = jnp.where(even, sent[1], sent[0])
-
-
-def widen_kernel(parity, field, got_near, got_far, wide_far, near, far, wide, sems):
+    near[0:256, :] = jnp.where(even, sent[0][0], sent[1][0])
+    near[256:272, :] = jnp.where(even, sent[0][1], sent[1][1])
+    far[0:256, :] = jnp.where(even, sent[1][0], sent[0][0])
+    far[256:272, :] = jnp.where(even, sent[1][1], sent[0][1])
+
+
+def widen_kernel(parity, field, got_near, got_far, near, far, wide):
     lane = lanes((512, 128))
     even = parity[0] == 0
     before = jnp.where(even, got_far[...], got_near[...])
     after = jnp.where(even, got_near[...], got_far[...])
-    copies = []
+    layers = [jnp.concatenate([v[0:256], roll(v[0:256], 64)], axis=0) for v in (before, after)]
+    faces = [
+        jnp.concatenate([roll(v[256:272], -32 * q) for q in range(4)], axis=0)
+        for v in (before, after)
+    ]
+    narrow = lanes((64, 128))
     for ex in range(EXL):
         own = roll(field[:, ex // 2 * 128 : ex // 2 * 128 + 128], 32 - ex % 2 * 64)
-        value = jnp.where(lane < 32, roll(before, -32 * ex), own)
-        value = jnp.where(lane < 96, value, roll(after, 96 - 32 * ex))
-        part = pl.ds(ex * 512, 512)
-        wide[part, :] = value
-        copies.append(pltpu.make_async_copy(wide.at[part], wide_far.at[part], sems.at[ex]))
-        copies[ex].start()
+        value = jnp.where(lane < 32, roll(layers[0], 16 - 16 * ex), own)
+        value = jnp.where(lane < 96, value, roll(layers[1], 96 - 16 * ex))
+        value = jnp.where((lane >= 16) & (lane < 112), value, 0.0)
+        wide[ex * 512 : ex * 512 + 512, :] = value
+        at = pl.ds(ex * 512 + 7, 64, stride=8)
+        inside = (narrow >= 8) & (narrow < 16)
+        wide[at, :] = jnp.where(inside, roll(faces[0], 8 - 8 * ex), wide[at, :])
+        at = pl.ds(ex * 512, 64, stride=8)
+        inside = (narrow >= 112) & (narrow < 120)
+        wide[at, :] = jnp.where(inside, roll(faces[1], 112 - 8 * ex), wide[at, :])
 
     def send(up, down):
         up[0:1024, :] = wide[1024:2048, :]
@@ -195,8 +221,6 @@
 
     pl.when(parity[1] == 0)(lambda: send(near, far))
     pl.when(parity[1] != 0)(lambda: send(far, near))
-    for copy in copies:
-        copy.wait()
 
 
 def pair_step(old, new, base, block_high, block_low):
@@ -260,17 +284,19 @@
 
 
 def first_step_kernel(
-    parity, wide, got_near, got_far, block_high, block_low, new, features_x, features_z, old, wall
+    parity, sent_near, sent_far, got_near, got_far, block_high, block_low,
+    new, features_x, features_z, old, wall,
 ):
-    def place(left, right):
+    def place(left, right, up, down):
         old[448:512, :] = left[1024:1088, :]
         old[512:1536, :] = left[0:1024, :]
+        old[1536:2560, :] = down[0:1024, :]
+        old[2560:3584, :] = up[0:1024, :]
         old[3584:4608, :] = right[0:1024, :]
         old[4608:4672, :] = right[1024:1088, :]
 
-    pl.when(parity[1] == 0)(lambda: place(got_far, got_near))
-    pl.when(parity[1] != 0)(lambda: place(got_near, got_far))
-    old[1536:3584, :] = wide[...]
+    pl.when(parity[1] == 0)(lambda: place(got_far, got_near, sent_near, sent_far))
+    pl.when(parity[1] != 0)(lambda: place(got_near, got_far, sent_far, sent_near))
 
     source = lax.broadcasted_iota(jnp.int32, (256, 128), 0)
     goal = lanes((256, 128)) % 32
@@ -416,7 +442,7 @@
 def finish_kernel(
     first, second, edges, features_own, features_x, features_z, grad,
     u, columns_y, plane_high, plane_low,
-    new_first, new_second, out, spread, state, grown,
+    new_first, new_second, out_far, spread, state, grown, out, sems,
 ):
     table = grad[...]
     weight = first[...].astype(F32)
@@ -481,6 +507,7 @@
             ],
             axis=0,
         )
+    copies = []
     for i in range(8):
         for j in range(8):
             at = i * 64 + j * 8
@@ -488,6 +515,11 @@
             for p in range(FLOW_STEPS):
                 value += columns_y[p * 8 + j : p * 8 + j + 1, :] * grown[p, i * 8 : i * 8 + 8, :]
             out[at : at + 8, :] = value
+        part = pl.ds(64 * i, 64)
+        copies.append(pltpu.make_async_copy(out.at[part], out_far.at[part], sems.at[i]))
+        copies[i].start()
+    for copy in copies:
+        copy.wait()
 
 
 VM = pl.BlockSpec(memory_space=pltpu.VMEM)
@@ -538,29 +570,27 @@
 
     counts, near, far = call(
         start_kernel,
-        [sds((64, 128)), sds((512, 128)), sds((512, 128))],
+        [sds((64, 128)), sds((272, 128)), sds((272, 128))],
         [
-            pltpu.VMEM((512, 256), F32),
+            pltpu.VMEM((1024, 128), F32),
             pltpu.VMEM((1, 64), jnp.int32),
-            pltpu.SemaphoreType.DMA((2,)),
+            pltpu.SemaphoreType.DMA((3,)),
         ],
         1,
         parity, field, route_row,
         arrays=HB,
-        limit=54500,
+        limit=60 * 1024,
     )
     near, far = swapped(near, far, "group")
     counts = lax.all_to_all(counts, "solver", 0, 0, tiled=True)
-    wide, near, far = call(
+    sent_near, sent_far = call(
         widen_kernel,
-        [sds((2048, 128)), sds((1088, 128)), sds((1088, 128))],
-        [pltpu.VMEM((2048, 128), F32), pltpu.SemaphoreType.DMA((4,))],
+        [sds((1088, 128)), sds((1088, 128))],
+        [pltpu.VMEM((2048, 128), F32)],
         1,
         parity, field, near, far,
-        results=[HB, VM, VM],
-        limit=52500,
     )
-    near, far = swapped(near, far, "solver")
+    near, far = swapped(sent_near, sent_far, "solver")
 
     grad, features = call(
         grad_kernel,
@@ -592,7 +622,7 @@
                 [state, sds((64, 256), BF), sds((64, 256), BF)],
                 [space, pltpu.VMEM((512, 128), F32)],
                 1,
-                parity, wide, near, far, block_high, block_low,
+                parity, sent_near, sent_far, near, far, block_high, block_low,
             )
         if number == 2:
             u = middle(middle(u, 1, 4), 2, 3)
@@ -609,10 +639,13 @@
             pltpu.VMEM((HID, 128), F32),
             pltpu.VMEM((64, 128), F32),
             pltpu.VMEM((FLOW_STEPS, 64, 256), F32),
+            pltpu.VMEM((512, 256), F32),
+            pltpu.SemaphoreType.DMA((8,)),
         ],
         0,
         first_weight, second_row, face_edges, features, features_x, features_z,
         grad, u, jnp.asarray(COLUMNS, F32), jnp.asarray(PLANE_HIGH), jnp.asarray(PLANE_LOW),
+        results=[VM, VM, HB],
     )
     return (new_field.reshape(8, 8, 8, 256), new_first, new_second.reshape(HID, 1))
 

time: 77.5 us -> 83.9 us (1.083)
  the two profiles are of different devices: /device:TPU:2 before, /device:TPU:1 now
where the time goes in v1:
time: 83.9 us; the launch traced here: 82.8 us
  starting transfers between devices  28.3 us (34%)
  Pallas kernels  26.2 us (31%)
  blocking collectives  18.1 us (22%)
  waiting for transfers between devices  8.37 us (10%)
  between operations  1.07 us (1%)
    pallas_call x9, Pallas kernels, call(): pl.pallas_call(kernel, out_shape=out_shape, in_specs=[SM] * scalars + [ar...  26.2 us
    all_to_all x1, blocking collectives, shards(): counts = lax.all_to_all(counts, 'solver', 0, 0, tiled=True)  18.1 us
    ppermute x12, starting transfers between devices, partners(): lax.ppermute(value, both, [(d, d ^ m << shift) for d in range(devices)])  17.6 us
    ppermute x4, starting transfers between devices, swapped(): return (lax.ppermute(near, axis, pairs), lax.ppermute(far, axis, others))  10.7 us
    ppermute x12, waiting for transfers between devices, partners(): lax.ppermute(value, both, [(d, d ^ m << shift) for d in range(devices)])  8.36 us
  transfers between devices with their start and end apart: 16, of which 4 were waited for; matrix products, arithmetic and copies ran while one was open for 0% of the time, Pallas kernels for 2%

profile of v1, /device:TPU:1, one launch (start us, length us, event | category | flops | bytes accessed | tf_op | source)
XLA Modules:
  0.0 82.8 jit_solution(2838358741928056005)
XLA Ops:
  1.3 3.2 %shard_map.130 = (f32[64,128]{1,0:T(8,128)}, f32[272,128]{1,0:T(8,128)}, f32[272,128]{1,0:T(8,128)}) custom-call(s32[2]{0:T(128)} %pad_add_fusion.parity, f32[512,256]{1,0:T(8,128)} %bitcast.13, s32[1,64]{1,0:T(1,128)} %bitcast.18), custom_call_target="tpu_custom_call" | custom-call | flops 4000000000 | bytes 1000000 | tf_op jit(solution)/shard_map/pallas_call | solution.py:535
  4.6 18.1 %all_to_all.11 = f32[64,1,128]{2,1,0:T(1,128)S(1)} all-to-all(f32[64,1,128]{2,1,0:T(1,128)} %bitcast.21), channel_id=1, replica_groups=mesh['solver'=64,'group'=4] {'solver'}, dimensions={0} | all-to-all | bytes 65536 | tf_op jit(solution)/shard_map/all_to_all | solution.py:585
  22.7 3.5 %shard_map.131 = (f32[8,1024]{1,0:T(8,128)S(1)}, bf16[64,256]{1,0:T(8,128)(2,1)S(1)}) custom-call(f32[512,256]{1,0:T(8,128)S(1)} %bitcast.14, bf16[8,1024]{1,0:T(8,128)(2,1)S(1)} %copy-done.1, bf16[1,1024]{1,0:T(2,128)(2,1)S(1)} %bitcast.16, s32[2,256]{1,0:T(2,128)S(1)} %copy-done.3, s32[1,64]{1,0:T(1,128)S(1)} %bitcast.19, s32[1,64]{1,0:T(1,128)S(1)} %bitcast.20, ...), custom_call_target="tpu_custom_call" | custom-call | flops 4000000000 | bytes 1000000 | tf_op jit(solution)/shard_map/pallas_call | solution.py:535
  26.6 1.6 %collective-permute-start.5 = (f32[8,1024]{1,0:T(8,128)S(1)}, f32[8,1024]{1,0:T(8,128)S(1)}, u32[]{:S(2)}, u32[]{:S(2)}) collective-permute-start(f32[8,1024]{1,0:T(8,128)S(1)} %get-tuple-element.24), channel_id=1, source_target_pairs={{0,128},{1,129},{2,130},{3,131},{4,132},{5,133},{6,134},{7,135},{8... | collective-permute-start | bytes 98312 | tf_op jit(solution)/shard_map/ppermute | solution.py:553
  28.2 1.9 %collective-permute-start.6 = (f32[8,1024]{1,0:T(8,128)S(1)}, f32[8,1024]{1,0:T(8,128)S(1)}, u32[]{:S(2)}, u32[]{:S(2)}) collective-permute-start(f32[8,1024]{1,0:T(8,128)S(1)} %get-tuple-element.24), channel_id=1, source_target_pairs={{0,192},{1,193},{2,194},{3,195},{4,196},{5,197},{6,198},{7,199},{8... | collective-permute-start | bytes 98312 | tf_op jit(solution)/shard_map/ppermute | solution.py:553
  30.1 3.0 %collective-permute-start = (f32[272,128]{1,0:T(8,128)S(1)}, f32[272,128]{1,0:T(8,128)S(1)}, u32[]{:S(2)}, u32[]{:S(2)}) collective-permute-start(f32[272,128]{1,0:T(8,128)S(1)} %copy-done.13), channel_id=1, source_target_pairs={{0,1},{1,0},{2,3},{3,2},{4,5},{5,4},{6,7},{7,6},{8,9},{9,8},{10,11... | collective-permute-start | bytes 417800 | tf_op jit(solution)/shard_map/ppermute | solution.py:561
  33.1 3.3 %collective-permute-start.1 = (f32[272,128]{1,0:T(8,128)S(1)}, f32[272,128]{1,0:T(8,128)S(1)}, u32[]{:S(2)}, u32[]{:S(2)}) collective-permute-start(f32[272,128]{1,0:T(8,128)S(1)} %copy-done.12), channel_id=1, source_target_pairs={{0,3},{1,2},{2,1},{3,0},{4,7},{5,6},{6,5},{7,4},{8,11},{9,10},{10,... | collective-permute-start | bytes 417800 | tf_op jit(solution)/shard_map/ppermute | solution.py:561
  36.5 2.2 %collective-permute-start.7 = (f32[8,1024]{1,0:T(8,128)S(1)}, f32[8,1024]{1,0:T(8,128)S(1)}, u32[]{:S(2)}, u32[]{:S(2)}) collective-permute-start(f32[8,1024]{1,0:T(8,128)S(1)} %add_add_fusion.3), channel_id=1, source_target_pairs={{0,4},{1,5},{2,6},{3,7},{4,0},{5,1},{6,2},{7,3},{8,12},{9,13},{10,... | collective-permute-start | bytes 98312 | tf_op jit(solution)/shard_map/ppermute | solution.py:553
  39.0 1.5 %collective-permute-start.9 = (f32[8,1024]{1,0:T(8,128)S(1)}, f32[8,1024]{1,0:T(8,128)S(1)}, u32[]{:S(2)}, u32[]{:S(2)}) collective-permute-start(f32[8,1024]{1,0:T(8,128)S(1)} %add_add_fusion.3), channel_id=1, source_target_pairs={{0,12},{1,13},{2,14},{3,15},{4,8},{5,9},{6,10},{7,11},{8,4},{9,5},... | collective-permute-start | bytes 98312 | tf_op jit(solution)/shard_map/ppermute | solution.py:553
  40.5 1.6 %shard_map.132 = (f32[1088,128]{1,0:T(8,128)S(1)}, f32[1088,128]{1,0:T(8,128)S(1)}) custom-call(s32[2]{0:T(128)S(1)} %copy-done.11, f32[512,256]{1,0:T(8,128)S(1)} %bitcast.15, f32[272,128]{1,0:T(8,128)S(1)} %collective-permute-done.got_near, f32[272,128]{1,0:T(8,128)S(1)} %collective-permute-done.1.got_far), custom_call_target="tpu_custom_call" | custom-call | flops 4000000000 | bytes 1000000 | tf_op jit(solution)/shard_map/pallas_call | solution.py:535
  42.0 4.4 %collective-permute-start.2 = (f32[1088,128]{1,0:T(8,128)S(1)}, f32[1088,128]{1,0:T(8,128)S(1)}, u32[]{:S(2)}, u32[]{:S(2)}) collective-permute-start(f32[1088,128]{1,0:T(8,128)S(1)} %get-tuple-element.20.sent_near), channel_id=1, source_target_pairs={{0,4},{4,0},{8,12},{12,8},{16,20},{20,16},{24,28},{28,24},{32,36},... | collective-permute-start | bytes 1671176 | tf_op jit(solution)/shard_map/ppermute | solution.py:561
  46.9 1.9 %collective-permute-start.11 = (f32[8,1024]{1,0:T(8,128)S(1)}, f32[8,1024]{1,0:T(8,128)S(1)}, u32[]{:S(2)}, u32[]{:S(2)}) collective-permute-start(f32[8,1024]{1,0:T(8,128)S(1)} %add_add_fusion.2), channel_id=1, source_target_pairs={{0,32},{1,33},{2,34},{3,35},{4,36},{5,37},{6,38},{7,39},{8,40},{9,... | collective-permute-start | bytes 98312 | tf_op jit(solution)/shard_map/ppermute | solution.py:553
  48.8 1.7 %collective-permute-start.12 = (f32[8,1024]{1,0:T(8,128)S(1)}, f32[8,1024]{1,0:T(8,128)S(1)}, u32[]{:S(2)}, u32[]{:S(2)}) collective-permute-start(f32[8,1024]{1,0:T(8,128)S(1)} %add_add_fusion.2), channel_id=1, source_target_pairs={{0,48},{1,49},{2,50},{3,51},{4,52},{5,53},{6,54},{7,55},{8,56},{9,... | collective-permute-start | bytes 98312 | tf_op jit(solution)/shard_map/ppermute | solution.py:553
  51.5 2.0 %collective-permute-done.12 = f32[8,1024]{1,0:T(8,128)S(1)} collective-permute-done((f32[8,1024]{1,0:T(8,128)S(1)}, f32[8,1024]{1,0:T(8,128)S(1)}, u32[]{:S(2)}, u32[]{:S(2)}) %collective-permute-start.12) | collective-permute-done | bytes 32800 | tf_op jit(solution)/shard_map/ppermute | solution.py:553
  53.6 1.2 %collective-permute-start.13 = (f32[8,1024]{1,0:T(8,128)S(1)}, f32[8,1024]{1,0:T(8,128)S(1)}, u32[]{:S(2)}, u32[]{:S(2)}) collective-permute-start(f32[8,1024]{1,0:T(8,128)S(1)} %add_add_fusion.1), channel_id=1, source_target_pairs={{0,1},{1,0},{2,3},{3,2},{4,5},{5,4},{6,7},{7,6},{8,9},{9,8},{10,11... | collective-permute-start | bytes 98312 | tf_op jit(solution)/shard_map/ppermute | solution.py:553
  54.8 4.6 %collective-permute-start.14 = (f32[8,1024]{1,0:T(8,128)S(1)}, f32[8,1024]{1,0:T(8,128)S(1)}, u32[]{:S(2)}, u32[]{:S(2)}) collective-permute-start(f32[8,1024]{1,0:T(8,128)S(1)} %add_add_fusion.1), channel_id=1, source_target_pairs={{0,2},{1,3},{2,0},{3,1},{4,6},{5,7},{6,4},{7,5},{8,10},{9,11},{10,... | collective-permute-start | bytes 98312 | tf_op jit(solution)/shard_map/ppermute | solution.py:553
  59.3 4.1 %collective-permute-done.14 = f32[8,1024]{1,0:T(8,128)S(1)} collective-permute-done((f32[8,1024]{1,0:T(8,128)S(1)}, f32[8,1024]{1,0:T(8,128)S(1)}, u32[]{:S(2)}, u32[]{:S(2)}) %collective-permute-start.14) | collective-permute-done | bytes 32800 | tf_op jit(solution)/shard_map/ppermute | solution.py:553
  63.5 1.1 %collective-permute-done.15 = f32[8,1024]{1,0:T(8,128)S(1)} collective-permute-done((f32[8,1024]{1,0:T(8,128)S(1)}, f32[8,1024]{1,0:T(8,128)S(1)}, u32[]{:S(2)}, u32[]{:S(2)}) %collective-permute-start.15) | collective-permute-done | bytes 32800 | tf_op jit(solution)/shard_map/ppermute | solution.py:553
  64.6 3.6 %shard_map.133 = (f32[5120,128]{1,0:T(8,128)S(1)}, bf16[64,256]{1,0:T(8,128)(2,1)S(1)}, bf16[64,256]{1,0:T(8,128)(2,1)S(1)}) custom-call(s32[2]{0:T(128)S(1)} %copy-done.11, f32[1088,128]{1,0:T(8,128)S(1)} %get-tuple-element.20.sent_near, f32[1088,128]{1,0:T(8,128)S(1)} %get-tuple-element.21.sent_far, f32[1088,128]{1,0:T(8,128)S(1)} %collective-permute-done.2.got_near, ...), custom_call_target="tpu_custom_call" | custom-call | flops 4000000000 | bytes 1000000 | tf_op jit(solution)/shard_map/pallas_call | solution.py:535
  68.2 2.3 %shard_map.134.old = f32[5120,128]{1,0:T(8,128)S(1)} custom-call(f32[5120,128]{1,0:T(8,128)S(1)} %get-tuple-element.25.old, bf16[256,256]{1,0:T(8,128)(2,1)S(1)} %copy-done.6, bf16[256,256]{1,0:T(8,128)(2,1)S(1)} %copy-done.7), custom_call_target="tpu_custom_call" | custom-call | flops 4000000000 | bytes 1000000 | tf_op jit(solution)/shard_map/pallas_call | solution.py:535
  70.6 1.7 %shard_map.135.old = f32[5120,128]{1,0:T(8,128)S(1)} custom-call(f32[5120,128]{1,0:T(8,128)S(1)} %shard_map.134.old, bf16[256,256]{1,0:T(8,128)(2,1)S(1)} %copy-done.6, bf16[256,256]{1,0:T(8,128)(2,1)S(1)} %copy-done.7), custom_call_target="tpu_custom_call" | custom-call | flops 4000000000 | bytes 1000000 | tf_op jit(solution)/shard_map/pallas_call | solution.py:535
  72.3 1.7 %shard_map.136.old = f32[5120,128]{1,0:T(8,128)S(1)} custom-call(f32[5120,128]{1,0:T(8,128)S(1)} %shard_map.135.old, bf16[256,256]{1,0:T(8,128)(2,1)S(1)} %copy-done.6, bf16[256,256]{1,0:T(8,128)(2,1)S(1)} %copy-done.7), custom_call_target="tpu_custom_call" | custom-call | flops 4000000000 | bytes 1000000 | tf_op jit(solution)/shard_map/pallas_call | solution.py:535
  74.1 1.5 %shard_map.137.u = f32[512,256]{1,0:T(8,128)S(1)} custom-call(f32[5120,128]{1,0:T(8,128)S(1)} %shard_map.136.old, bf16[256,256]{1,0:T(8,128)(2,1)S(1)} %copy-done.6, bf16[256,256]{1,0:T(8,128)(2,1)S(1)} %copy-done.7), custom_call_target="tpu_custom_call" | custom-call | flops 4000000000 | bytes 1000000 | tf_op jit(solution)/shard_map/pallas_call | solution.py:535
  75.7 7.0 %shard_map.138 = (bf16[8,1024]{1,0:T(8,128)(2,1)}, bf16[1,1024]{1,0:T(2,128)(2,1)}, f32[512,256]{1,0:T(8,128)}) custom-call(bf16[8,1024]{1,0:T(8,128)(2,1)S(1)} %copy-done.1, bf16[1,1024]{1,0:T(2,128)(2,1)S(1)} %bitcast.17, s32[2,256]{1,0:T(2,128)S(1)} %copy-done.3, bf16[64,256]{1,0:T(8,128)(2,1)S(1)} %get-tuple-element.17.features_own, ...), custom_call_target="tpu_custom_call" | custom-call | flops 4000000000 | bytes 1000000 | tf_op jit(solution)/shard_map/pallas_call | solution.py:535
  (51 shorter events, 2.9 us)
Async XLA Ops:
  1.3 21.4 %copy-start = (f32[8,8,8,256]{3,2,1,0:T(8,128)S(1)}, f32[8,8,8,256]{3,2,1,0:T(8,128)}, u32[]{:S(2)}) copy-start(f32[8,8,8,256]{3,2,1,0:T(8,128)} %param.11) | copy-start | bytes 1572868
  1.3 21.4 %copy-start.1 = (bf16[8,1024]{1,0:T(8,128)(2,1)S(1)}, bf16[8,1024]{1,0:T(8,128)(2,1)}, u32[]{:S(2)}) copy-start(bf16[8,1024]{1,0:T(8,128)(2,1)} %first.3) | copy-start | bytes 49156
  1.3 21.4 %copy-start.2 = (bf16[1024,1]{0,1:T(2,128)(2,1)S(1)}, bf16[1024,1]{0,1:T(2,128)(2,1)}, u32[]{:S(2)}) copy-start(bf16[1024,1]{0,1:T(2,128)(2,1)} %param.13) | copy-start | bytes 6148
  1.3 21.4 %copy-start.3 = (s32[2,256]{1,0:T(2,128)S(1)}, s32[2,256]{1,0:T(2,128)}, u32[]{:S(2)}) copy-start(s32[2,256]{1,0:T(2,128)} %edges.3) | copy-start | bytes 6148
  1.3 21.4 %copy-start.4 = (s32[64,1]{0,1:T(1,128)S(1)}, s32[64,1]{0,1:T(1,128)}, u32[]{:S(2)}) copy-start(s32[64,1]{0,1:T(1,128)} %param.16) | copy-start | bytes 772
  1.3 21.4 %copy-start.5 = (s32[64]{0:T(128)S(1)}, s32[64]{0:T(128)}, u32[]{:S(2)}) copy-start(s32[64]{0:T(128)} %param.15) | copy-start | bytes 772
  26.3 10.2 %collective-permute-start.4 = (f32[8,1024]{1,0:T(8,128)S(1)}, f32[8,1024]{1,0:T(8,128)S(1)}, u32[]{:S(2)}, u32[]{:S(2)}) collective-permute-start(f32[8,1024]{1,0:T(8,128)S(1)} %get-tuple-element.24), channel_id=1, source_target_pairs={{0,64},{1,65},{2,66},{3,67},{4,68},{5,69},{6,70},{7,71},{8,72},{9,... | collective-permute-start | bytes 98312 | tf_op jit(solution)/shard_map/ppermute | solution.py:553
  26.6 9.8 %collective-permute-start.5 = (f32[8,1024]{1,0:T(8,128)S(1)}, f32[8,1024]{1,0:T(8,128)S(1)}, u32[]{:S(2)}, u32[]{:S(2)}) collective-permute-start(f32[8,1024]{1,0:T(8,128)S(1)} %get-tuple-element.24), channel_id=1, source_target_pairs={{0,128},{1,129},{2,130},{3,131},{4,132},{5,133},{6,134},{7,135},{8... | collective-permute-start | bytes 98312 | tf_op jit(solution)/shard_map/ppermute | solution.py:553
  28.2 8.2 %collective-permute-start.6 = (f32[8,1024]{1,0:T(8,128)S(1)}, f32[8,1024]{1,0:T(8,128)S(1)}, u32[]{:S(2)}, u32[]{:S(2)}) collective-permute-start(f32[8,1024]{1,0:T(8,128)S(1)} %get-tuple-element.24), channel_id=1, source_target_pairs={{0,192},{1,193},{2,194},{3,195},{4,196},{5,197},{6,198},{7,199},{8... | collective-permute-start | bytes 98312 | tf_op jit(solution)/shard_map/ppermute | solution.py:553
  30.1 10.3 %collective-permute-start = (f32[272,128]{1,0:T(8,128)S(1)}, f32[272,128]{1,0:T(8,128)S(1)}, u32[]{:S(2)}, u32[]{:S(2)}) collective-permute-start(f32[272,128]{1,0:T(8,128)S(1)} %copy-done.13), channel_id=1, source_target_pairs={{0,1},{1,0},{2,3},{3,2},{4,5},{5,4},{6,7},{7,6},{8,9},{9,8},{10,11... | collective-permute-start | bytes 417800 | tf_op jit(solution)/shard_map/ppermute | solution.py:561
  33.1 7.3 %collective-permute-start.1 = (f32[272,128]{1,0:T(8,128)S(1)}, f32[272,128]{1,0:T(8,128)S(1)}, u32[]{:S(2)}, u32[]{:S(2)}) collective-permute-start(f32[272,128]{1,0:T(8,128)S(1)} %copy-done.12), channel_id=1, source_target_pairs={{0,3},{1,2},{2,1},{3,0},{4,7},{5,6},{6,5},{7,4},{8,11},{9,10},{10,... | collective-permute-start | bytes 417800 | tf_op jit(solution)/shard_map/ppermute | solution.py:561
  36.5 28.1 %copy-start.6 = (bf16[256,256]{1,0:T(8,128)(2,1)S(1)}, bf16[256,256]{1,0:T(8,128)(2,1)}, u32[]{:S(2)}) copy-start(bf16[256,256]{1,0:T(8,128)(2,1)} %constant.21.clone.block_high) | copy-start | bytes 393220
  36.5 28.1 %copy-start.7 = (bf16[256,256]{1,0:T(8,128)(2,1)S(1)}, bf16[256,256]{1,0:T(8,128)(2,1)}, u32[]{:S(2)}) copy-start(bf16[256,256]{1,0:T(8,128)(2,1)} %constant.22.clone.block_low) | copy-start | bytes 393220
  36.5 10.0 %collective-permute-start.7 = (f32[8,1024]{1,0:T(8,128)S(1)}, f32[8,1024]{1,0:T(8,128)S(1)}, u32[]{:S(2)}, u32[]{:S(2)}) collective-permute-start(f32[8,1024]{1,0:T(8,128)S(1)} %add_add_fusion.3), channel_id=1, source_target_pairs={{0,4},{1,5},{2,6},{3,7},{4,0},{5,1},{6,2},{7,3},{8,12},{9,13},{10,... | collective-permute-start | bytes 98312 | tf_op jit(solution)/shard_map/ppermute | solution.py:553
  38.7 7.7 %collective-permute-start.8 = (f32[8,1024]{1,0:T(8,128)S(1)}, f32[8,1024]{1,0:T(8,128)S(1)}, u32[]{:S(2)}, u32[]{:S(2)}) collective-permute-start(f32[8,1024]{1,0:T(8,128)S(1)} %add_add_fusion.3), channel_id=1, source_target_pairs={{0,8},{1,9},{2,10},{3,11},{4,12},{5,13},{6,14},{7,15},{8,0},{9,1},... | collective-permute-start | bytes 98312 | tf_op jit(solution)/shard_map/ppermute | solution.py:553
  39.0 7.5 %collective-permute-start.9 = (f32[8,1024]{1,0:T(8,128)S(1)}, f32[8,1024]{1,0:T(8,128)S(1)}, u32[]{:S(2)}, u32[]{:S(2)}) collective-permute-start(f32[8,1024]{1,0:T(8,128)S(1)} %add_add_fusion.3), channel_id=1, source_target_pairs={{0,12},{1,13},{2,14},{3,15},{4,8},{5,9},{6,10},{7,11},{8,4},{9,5},... | collective-permute-start | bytes 98312 | tf_op jit(solution)/shard_map/ppermute | solution.py:553
  42.0 22.5 %collective-permute-start.2 = (f32[1088,128]{1,0:T(8,128)S(1)}, f32[1088,128]{1,0:T(8,128)S(1)}, u32[]{:S(2)}, u32[]{:S(2)}) collective-permute-start(f32[1088,128]{1,0:T(8,128)S(1)} %get-tuple-element.20.sent_near), channel_id=1, source_target_pairs={{0,4},{4,0},{8,12},{12,8},{16,20},{20,16},{24,28},{28,24},{32,36},... | collective-permute-start | bytes 1671176 | tf_op jit(solution)/shard_map/ppermute | solution.py:561
  46.5 18.1 %collective-permute-start.3 = (f32[1088,128]{1,0:T(8,128)S(1)}, f32[1088,128]{1,0:T(8,128)S(1)}, u32[]{:S(2)}, u32[]{:S(2)}) collective-permute-start(f32[1088,128]{1,0:T(8,128)S(1)} %get-tuple-element.21.sent_far), channel_id=1, source_target_pairs={{0,252},{4,8},{8,4},{12,16},{16,12},{20,24},{24,20},{28,32},{32,28... | collective-permute-start | bytes 1671176 | tf_op jit(solution)/shard_map/ppermute | solution.py:561
  46.5 4.0 %collective-permute-start.10 = (f32[8,1024]{1,0:T(8,128)S(1)}, f32[8,1024]{1,0:T(8,128)S(1)}, u32[]{:S(2)}, u32[]{:S(2)}) collective-permute-start(f32[8,1024]{1,0:T(8,128)S(1)} %add_add_fusion.2), channel_id=1, source_target_pairs={{0,16},{1,17},{2,18},{3,19},{4,20},{5,21},{6,22},{7,23},{8,24},{9,... | collective-permute-start | bytes 98312 | tf_op jit(solution)/shard_map/ppermute | solution.py:553
  46.9 4.6 %collective-permute-start.11 = (f32[8,1024]{1,0:T(8,128)S(1)}, f32[8,1024]{1,0:T(8,128)S(1)}, u32[]{:S(2)}, u32[]{:S(2)}) collective-permute-start(f32[8,1024]{1,0:T(8,128)S(1)} %add_add_fusion.2), channel_id=1, source_target_pairs={{0,32},{1,33},{2,34},{3,35},{4,36},{5,37},{6,38},{7,39},{8,40},{9,... | collective-permute-start | bytes 98312 | tf_op jit(solution)/shard_map/ppermute | solution.py:553
  48.8 4.8 %collective-permute-start.12 = (f32[8,1024]{1,0:T(8,128)S(1)}, f32[8,1024]{1,0:T(8,128)S(1)}, u32[]{:S(2)}, u32[]{:S(2)}) collective-permute-start(f32[8,1024]{1,0:T(8,128)S(1)} %add_add_fusion.2), channel_id=1, source_target_pairs={{0,48},{1,49},{2,50},{3,51},{4,52},{5,53},{6,54},{7,55},{8,56},{9,... | collective-permute-start | bytes 98312 | tf_op jit(solution)/shard_map/ppermute | solution.py:553
  53.6 5.8 %collective-permute-start.13 = (f32[8,1024]{1,0:T(8,128)S(1)}, f32[8,1024]{1,0:T(8,128)S(1)}, u32[]{:S(2)}, u32[]{:S(2)}) collective-permute-start(f32[8,1024]{1,0:T(8,128)S(1)} %add_add_fusion.1), channel_id=1, source_target_pairs={{0,1},{1,0},{2,3},{3,2},{4,5},{5,4},{6,7},{7,6},{8,9},{9,8},{10,11... | collective-permute-start | bytes 98312 | tf_op jit(solution)/shard_map/ppermute | solution.py:553
  54.8 8.7 %collective-permute-start.14 = (f32[8,1024]{1,0:T(8,128)S(1)}, f32[8,1024]{1,0:T(8,128)S(1)}, u32[]{:S(2)}, u32[]{:S(2)}) collective-permute-start(f32[8,1024]{1,0:T(8,128)S(1)} %add_add_fusion.1), channel_id=1, source_target_pairs={{0,2},{1,3},{2,0},{3,1},{4,6},{5,7},{6,4},{7,5},{8,10},{9,11},{10,... | collective-permute-start | bytes 98312 | tf_op jit(solution)/shard_map/ppermute | solution.py:553
  59.3 5.2 %collective-permute-start.15 = (f32[8,1024]{1,0:T(8,128)S(1)}, f32[8,1024]{1,0:T(8,128)S(1)}, u32[]{:S(2)}, u32[]{:S(2)}) collective-permute-start(f32[8,1024]{1,0:T(8,128)S(1)} %add_add_fusion.1), channel_id=1, source_target_pairs={{0,3},{1,2},{2,1},{3,0},{4,7},{5,6},{6,5},{7,4},{8,11},{9,10},{10,... | collective-permute-start | bytes 98312 | tf_op jit(solution)/shard_map/ppermute | solution.py:553
  (6 other events, 40.2 us)

commit v2 on v1

--- a/solution.py
+++ b/solution.py
@@ -442,7 +442,7 @@
 def finish_kernel(
     first, second, edges, features_own, features_x, features_z, grad,
     u, columns_y, plane_high, plane_low,
-    new_first, new_second, out_far, spread, state, grown, out, sems,
+    new_first, new_second, out, spread, state, grown,
 ):
     table = grad[...]
     weight = first[...].astype(F32)
@@ -507,7 +507,6 @@
             ],
             axis=0,
         )
-    copies = []
     for i in range(8):
         for j in range(8):
             at = i * 64 + j * 8
@@ -515,11 +514,6 @@
             for p in range(FLOW_STEPS):
                 value += columns_y[p * 8 + j : p * 8 + j + 1, :] * grown[p, i * 8 : i * 8 + 8, :]
             out[at : at + 8, :] = value
-        part = pl.ds(64 * i, 64)
-        copies.append(pltpu.make_async_copy(out.at[part], out_far.at[part], sems.at[i]))
-        copies[i].start()
-    for copy in copies:
-        copy.wait()
 
 
 VM = pl.BlockSpec(memory_space=pltpu.VMEM)
@@ -579,7 +573,7 @@
         1,
         parity, field, route_row,
         arrays=HB,
-        limit=60 * 1024,
+        limit=54500,
     )
     near, far = swapped(near, far, "group")
     counts = lax.all_to_all(counts, "solver", 0, 0, tiled=True)
@@ -639,13 +633,10 @@
             pltpu.VMEM((HID, 128), F32),
             pltpu.VMEM((64, 128), F32),
             pltpu.VMEM((FLOW_STEPS, 64, 256), F32),
-            pltpu.VMEM((512, 256), F32),
-            pltpu.SemaphoreType.DMA((8,)),
         ],
         0,
         first_weight, second_row, face_edges, features, features_x, features_z,
         grad, u, jnp.asarray(COLUMNS, F32), jnp.asarray(PLANE_HIGH), jnp.asarray(PLANE_LOW),
-        results=[VM, VM, HB],
     )
     return (new_field.reshape(8, 8, 8, 256), new_first, new_second.reshape(HID, 1))
 

time: 83.9 us -> 82.1 us (0.979)
  Pallas kernels: 26.2 us -> 24.6 us
    pallas_call x9, Pallas kernels: 26.2 us -> 24.6 us  [call(): pl.pallas_call(kernel, out_shape=out_shape, in_specs=[SM] * scalars + [ar...]
where the time goes in v2:
time: 82.1 us; the launch traced here: 81.1 us
  starting transfers between devices  28.5 us (35%)
  Pallas kernels  24.6 us (30%)
  blocking collectives  17.9 us (22%)
  waiting for transfers between devices  8.35 us (10%)
  between operations  0.86 us (1%)
    pallas_call x9, Pallas kernels, call(): pl.pallas_call(kernel, out_shape=out_shape, in_specs=[SM] * scalars + [ar...  24.6 us
    all_to_all x1, blocking collectives, shards(): counts = lax.all_to_all(counts, 'solver', 0, 0, tiled=True)  17.9 us
    ppermute x12, starting transfers between devices, partners(): lax.ppermute(value, both, [(d, d ^ m << shift) for d in range(devices)])  17.7 us
    ppermute x4, starting transfers between devices, swapped(): return (lax.ppermute(near, axis, pairs), lax.ppermute(far, axis, others))  10.7 us
    ppermute x12, waiting for transfers between devices, partners(): lax.ppermute(value, both, [(d, d ^ m << shift) for d in range(devices)])  8.34 us
  transfers between devices with their start and end apart: 16, of which 4 were waited for; matrix products, arithmetic and copies ran while one was open for 0% of the time, Pallas kernels for 2%

profile of v2, /device:TPU:1, one launch (start us, length us, event | category | flops | bytes accessed | tf_op | source)
XLA Modules:
  0.0 81.1 jit_solution(16964068291627265944)
XLA Ops:
  1.4 2.3 %shard_map.130 = (f32[64,128]{1,0:T(8,128)S(1)}, f32[272,128]{1,0:T(8,128)S(1)}, f32[272,128]{1,0:T(8,128)S(1)}) custom-call(s32[2]{0:T(128)S(1)} %pad_add_fusion.parity, f32[512,256]{1,0:T(8,128)} %bitcast.14, s32[1,64]{1,0:T(1,128)S(1)} %bitcast.19), custom_call_target="tpu_custom_call" | custom-call | flops 4000000000 | bytes 1000000 | tf_op jit(solution)/shard_map/pallas_call | solution.py:529
  3.7 17.9 %all_to_all.11 = f32[64,1,128]{2,1,0:T(1,128)S(1)} all-to-all(f32[64,1,128]{2,1,0:T(1,128)S(1)} %bitcast.12), channel_id=1, replica_groups=mesh['solver'=64,'group'=4] {'solver'}, dimensions={0} | all-to-all | bytes 65536 | tf_op jit(solution)/shard_map/all_to_all | solution.py:579
  21.6 3.5 %shard_map.131 = (f32[8,1024]{1,0:T(8,128)S(1)}, bf16[64,256]{1,0:T(8,128)(2,1)S(1)}) custom-call(f32[512,256]{1,0:T(8,128)S(1)} %bitcast.15, bf16[8,1024]{1,0:T(8,128)(2,1)S(1)} %copy-done.1, bf16[1,1024]{1,0:T(2,128)(2,1)S(1)} %bitcast.17, s32[2,256]{1,0:T(2,128)S(1)} %copy-done.3, s32[1,64]{1,0:T(1,128)S(1)} %bitcast.20, s32[1,64]{1,0:T(1,128)S(1)} %bitcast.21, ...), custom_call_target="tpu_custom_call" | custom-call | flops 4000000000 | bytes 1000000 | tf_op jit(solution)/shard_map/pallas_call | solution.py:529
  25.5 1.6 %collective-permute-start.5 = (f32[8,1024]{1,0:T(8,128)S(1)}, f32[8,1024]{1,0:T(8,128)S(1)}, u32[]{:S(2)}, u32[]{:S(2)}) collective-permute-start(f32[8,1024]{1,0:T(8,128)S(1)} %get-tuple-element.24), channel_id=1, source_target_pairs={{0,128},{1,129},{2,130},{3,131},{4,132},{5,133},{6,134},{7,135},{8... | collective-permute-start | bytes 98312 | tf_op jit(solution)/shard_map/ppermute | solution.py:547
  27.1 1.9 %collective-permute-start.6 = (f32[8,1024]{1,0:T(8,128)S(1)}, f32[8,1024]{1,0:T(8,128)S(1)}, u32[]{:S(2)}, u32[]{:S(2)}) collective-permute-start(f32[8,1024]{1,0:T(8,128)S(1)} %get-tuple-element.24), channel_id=1, source_target_pairs={{0,192},{1,193},{2,194},{3,195},{4,196},{5,197},{6,198},{7,199},{8... | collective-permute-start | bytes 98312 | tf_op jit(solution)/shard_map/ppermute | solution.py:547
  29.0 3.0 %collective-permute-start = (f32[272,128]{1,0:T(8,128)S(1)}, f32[272,128]{1,0:T(8,128)S(1)}, u32[]{:S(2)}, u32[]{:S(2)}) collective-permute-start(f32[272,128]{1,0:T(8,128)S(1)} %get-tuple-element.18), channel_id=1, source_target_pairs={{0,1},{1,0},{2,3},{3,2},{4,5},{5,4},{6,7},{7,6},{8,9},{9,8},{10,11... | collective-permute-start | bytes 417800 | tf_op jit(solution)/shard_map/ppermute | solution.py:555
  32.0 3.3 %collective-permute-start.1 = (f32[272,128]{1,0:T(8,128)S(1)}, f32[272,128]{1,0:T(8,128)S(1)}, u32[]{:S(2)}, u32[]{:S(2)}) collective-permute-start(f32[272,128]{1,0:T(8,128)S(1)} %get-tuple-element.19), channel_id=1, source_target_pairs={{0,3},{1,2},{2,1},{3,0},{4,7},{5,6},{6,5},{7,4},{8,11},{9,10},{10,... | collective-permute-start | bytes 417800 | tf_op jit(solution)/shard_map/ppermute | solution.py:555
  35.3 2.2 %collective-permute-start.7 = (f32[8,1024]{1,0:T(8,128)S(1)}, f32[8,1024]{1,0:T(8,128)S(1)}, u32[]{:S(2)}, u32[]{:S(2)}) collective-permute-start(f32[8,1024]{1,0:T(8,128)S(1)} %add_add_fusion.3), channel_id=1, source_target_pairs={{0,4},{1,5},{2,6},{3,7},{4,0},{5,1},{6,2},{7,3},{8,12},{9,13},{10,... | collective-permute-start | bytes 98312 | tf_op jit(solution)/shard_map/ppermute | solution.py:547
  37.8 1.5 %collective-permute-start.9 = (f32[8,1024]{1,0:T(8,128)S(1)}, f32[8,1024]{1,0:T(8,128)S(1)}, u32[]{:S(2)}, u32[]{:S(2)}) collective-permute-start(f32[8,1024]{1,0:T(8,128)S(1)} %add_add_fusion.3), channel_id=1, source_target_pairs={{0,12},{1,13},{2,14},{3,15},{4,8},{5,9},{6,10},{7,11},{8,4},{9,5},... | collective-permute-start | bytes 98312 | tf_op jit(solution)/shard_map/ppermute | solution.py:547
  39.3 1.6 %shard_map.132 = (f32[1088,128]{1,0:T(8,128)S(1)}, f32[1088,128]{1,0:T(8,128)S(1)}) custom-call(s32[2]{0:T(128)S(1)} %pad_add_fusion.parity, f32[512,256]{1,0:T(8,128)S(1)} %bitcast.16, f32[272,128]{1,0:T(8,128)S(1)} %collective-permute-done.got_near, f32[272,128]{1,0:T(8,128)S(1)} %collective-permute-done.1.got_far), custom_call_target="tpu_custom_call" | custom-call | flops 4000000000 | bytes 1000000 | tf_op jit(solution)/shard_map/pallas_call | solution.py:529
  40.9 4.4 %collective-permute-start.2 = (f32[1088,128]{1,0:T(8,128)S(1)}, f32[1088,128]{1,0:T(8,128)S(1)}, u32[]{:S(2)}, u32[]{:S(2)}) collective-permute-start(f32[1088,128]{1,0:T(8,128)S(1)} %get-tuple-element.20.sent_near), channel_id=1, source_target_pairs={{0,4},{4,0},{8,12},{12,8},{16,20},{20,16},{24,28},{28,24},{32,36},... | collective-permute-start | bytes 1671176 | tf_op jit(solution)/shard_map/ppermute | solution.py:555
  45.8 1.9 %collective-permute-start.11 = (f32[8,1024]{1,0:T(8,128)S(1)}, f32[8,1024]{1,0:T(8,128)S(1)}, u32[]{:S(2)}, u32[]{:S(2)}) collective-permute-start(f32[8,1024]{1,0:T(8,128)S(1)} %add_add_fusion.2), channel_id=1, source_target_pairs={{0,32},{1,33},{2,34},{3,35},{4,36},{5,37},{6,38},{7,39},{8,40},{9,... | collective-permute-start | bytes 98312 | tf_op jit(solution)/shard_map/ppermute | solution.py:547
  47.6 1.7 %collective-permute-start.12 = (f32[8,1024]{1,0:T(8,128)S(1)}, f32[8,1024]{1,0:T(8,128)S(1)}, u32[]{:S(2)}, u32[]{:S(2)}) collective-permute-start(f32[8,1024]{1,0:T(8,128)S(1)} %add_add_fusion.2), channel_id=1, source_target_pairs={{0,48},{1,49},{2,50},{3,51},{4,52},{5,53},{6,54},{7,55},{8,56},{9,... | collective-permute-start | bytes 98312 | tf_op jit(solution)/shard_map/ppermute | solution.py:547
  50.4 2.0 %collective-permute-done.12 = f32[8,1024]{1,0:T(8,128)S(1)} collective-permute-done((f32[8,1024]{1,0:T(8,128)S(1)}, f32[8,1024]{1,0:T(8,128)S(1)}, u32[]{:S(2)}, u32[]{:S(2)}) %collective-permute-start.12) | collective-permute-done | bytes 32800 | tf_op jit(solution)/shard_map/ppermute | solution.py:547
  52.4 1.4 %collective-permute-start.13 = (f32[8,1024]{1,0:T(8,128)S(1)}, f32[8,1024]{1,0:T(8,128)S(1)}, u32[]{:S(2)}, u32[]{:S(2)}) collective-permute-start(f32[8,1024]{1,0:T(8,128)S(1)} %add_add_fusion.1), channel_id=1, source_target_pairs={{0,1},{1,0},{2,3},{3,2},{4,5},{5,4},{6,7},{7,6},{8,9},{9,8},{10,11... | collective-permute-start | bytes 98312 | tf_op jit(solution)/shard_map/ppermute | solution.py:547
  53.8 4.6 %collective-permute-start.14 = (f32[8,1024]{1,0:T(8,128)S(1)}, f32[8,1024]{1,0:T(8,128)S(1)}, u32[]{:S(2)}, u32[]{:S(2)}) collective-permute-start(f32[8,1024]{1,0:T(8,128)S(1)} %add_add_fusion.1), channel_id=1, source_target_pairs={{0,2},{1,3},{2,0},{3,1},{4,6},{5,7},{6,4},{7,5},{8,10},{9,11},{10,... | collective-permute-start | bytes 98312 | tf_op jit(solution)/shard_map/ppermute | solution.py:547
  58.4 4.0 %collective-permute-done.14 = f32[8,1024]{1,0:T(8,128)S(1)} collective-permute-done((f32[8,1024]{1,0:T(8,128)S(1)}, f32[8,1024]{1,0:T(8,128)S(1)}, u32[]{:S(2)}, u32[]{:S(2)}) %collective-permute-start.14) | collective-permute-done | bytes 32800 | tf_op jit(solution)/shard_map/ppermute | solution.py:547
  62.3 1.2 %collective-permute-done.15 = f32[8,1024]{1,0:T(8,128)S(1)} collective-permute-done((f32[8,1024]{1,0:T(8,128)S(1)}, f32[8,1024]{1,0:T(8,128)S(1)}, u32[]{:S(2)}, u32[]{:S(2)}) %collective-permute-start.15) | collective-permute-done | bytes 32800 | tf_op jit(solution)/shard_map/ppermute | solution.py:547
  63.6 3.6 %shard_map.133 = (f32[5120,128]{1,0:T(8,128)S(1)}, bf16[64,256]{1,0:T(8,128)(2,1)S(1)}, bf16[64,256]{1,0:T(8,128)(2,1)S(1)}) custom-call(s32[2]{0:T(128)S(1)} %pad_add_fusion.parity, f32[1088,128]{1,0:T(8,128)S(1)} %get-tuple-element.20.sent_near, f32[1088,128]{1,0:T(8,128)S(1)} %get-tuple-element.21.sent_far, ...), custom_call_target="tpu_custom_call" | custom-call | flops 4000000000 | bytes 1000000 | tf_op jit(solution)/shard_map/pallas_call | solution.py:529
  67.3 2.3 %shard_map.134.old = f32[5120,128]{1,0:T(8,128)S(1)} custom-call(f32[5120,128]{1,0:T(8,128)S(1)} %get-tuple-element.25.old, bf16[256,256]{1,0:T(8,128)(2,1)S(1)} %copy-done.6, bf16[256,256]{1,0:T(8,128)(2,1)S(1)} %copy-done.7), custom_call_target="tpu_custom_call" | custom-call | flops 4000000000 | bytes 1000000 | tf_op jit(solution)/shard_map/pallas_call | solution.py:529
  69.6 1.7 %shard_map.135.old = f32[5120,128]{1,0:T(8,128)S(1)} custom-call(f32[5120,128]{1,0:T(8,128)S(1)} %shard_map.134.old, bf16[256,256]{1,0:T(8,128)(2,1)S(1)} %copy-done.6, bf16[256,256]{1,0:T(8,128)(2,1)S(1)} %copy-done.7), custom_call_target="tpu_custom_call" | custom-call | flops 4000000000 | bytes 1000000 | tf_op jit(solution)/shard_map/pallas_call | solution.py:529
  71.4 1.7 %shard_map.136.old = f32[5120,128]{1,0:T(8,128)S(1)} custom-call(f32[5120,128]{1,0:T(8,128)S(1)} %shard_map.135.old, bf16[256,256]{1,0:T(8,128)(2,1)S(1)} %copy-done.6, bf16[256,256]{1,0:T(8,128)(2,1)S(1)} %copy-done.7), custom_call_target="tpu_custom_call" | custom-call | flops 4000000000 | bytes 1000000 | tf_op jit(solution)/shard_map/pallas_call | solution.py:529
  73.1 1.5 %shard_map.137.u = f32[512,256]{1,0:T(8,128)S(1)} custom-call(f32[5120,128]{1,0:T(8,128)S(1)} %shard_map.136.old, bf16[256,256]{1,0:T(8,128)(2,1)S(1)} %copy-done.6, bf16[256,256]{1,0:T(8,128)(2,1)S(1)} %copy-done.7), custom_call_target="tpu_custom_call" | custom-call | flops 4000000000 | bytes 1000000 | tf_op jit(solution)/shard_map/pallas_call | solution.py:529
  74.7 6.4 %shard_map.138 = (bf16[8,1024]{1,0:T(8,128)(2,1)}, bf16[1,1024]{1,0:T(2,128)(2,1)}, f32[512,256]{1,0:T(8,128)}) custom-call(bf16[8,1024]{1,0:T(8,128)(2,1)S(1)} %copy-done.1, bf16[1,1024]{1,0:T(2,128)(2,1)S(1)} %bitcast.18, s32[2,256]{1,0:T(2,128)S(1)} %copy-done.3, bf16[64,256]{1,0:T(8,128)(2,1)S(1)} %get-tuple-element.17.features_own, ...), custom_call_target="tpu_custom_call" | custom-call | flops 4000000000 | bytes 1000000 | tf_op jit(solution)/shard_map/pallas_call | solution.py:529
  (45 shorter events, 3.0 us)
Async XLA Ops:
  1.4 20.2 %copy-start = (f32[8,8,8,256]{3,2,1,0:T(8,128)S(1)}, f32[8,8,8,256]{3,2,1,0:T(8,128)}, u32[]{:S(2)}) copy-start(f32[8,8,8,256]{3,2,1,0:T(8,128)} %param.11) | copy-start | bytes 1572868
  1.4 20.2 %copy-start.1 = (bf16[8,1024]{1,0:T(8,128)(2,1)S(1)}, bf16[8,1024]{1,0:T(8,128)(2,1)}, u32[]{:S(2)}) copy-start(bf16[8,1024]{1,0:T(8,128)(2,1)} %first.3) | copy-start | bytes 49156
  1.4 20.2 %copy-start.2 = (bf16[1024,1]{0,1:T(2,128)(2,1)S(1)}, bf16[1024,1]{0,1:T(2,128)(2,1)}, u32[]{:S(2)}) copy-start(bf16[1024,1]{0,1:T(2,128)(2,1)} %param.13) | copy-start | bytes 6148
  1.4 20.2 %copy-start.3 = (s32[2,256]{1,0:T(2,128)S(1)}, s32[2,256]{1,0:T(2,128)}, u32[]{:S(2)}) copy-start(s32[2,256]{1,0:T(2,128)} %edges.3) | copy-start | bytes 6148
  1.4 20.2 %copy-start.5 = (s32[64]{0:T(128)S(1)}, s32[64]{0:T(128)}, u32[]{:S(2)}) copy-start(s32[64]{0:T(128)} %param.15) | copy-start | bytes 772
  25.1 10.2 %collective-permute-start.4 = (f32[8,1024]{1,0:T(8,128)S(1)}, f32[8,1024]{1,0:T(8,128)S(1)}, u32[]{:S(2)}, u32[]{:S(2)}) collective-permute-start(f32[8,1024]{1,0:T(8,128)S(1)} %get-tuple-element.24), channel_id=1, source_target_pairs={{0,64},{1,65},{2,66},{3,67},{4,68},{5,69},{6,70},{7,71},{8,72},{9,... | collective-permute-start | bytes 98312 | tf_op jit(solution)/shard_map/ppermute | solution.py:547
  25.5 9.8 %collective-permute-start.5 = (f32[8,1024]{1,0:T(8,128)S(1)}, f32[8,1024]{1,0:T(8,128)S(1)}, u32[]{:S(2)}, u32[]{:S(2)}) collective-permute-start(f32[8,1024]{1,0:T(8,128)S(1)} %get-tuple-element.24), channel_id=1, source_target_pairs={{0,128},{1,129},{2,130},{3,131},{4,132},{5,133},{6,134},{7,135},{8... | collective-permute-start | bytes 98312 | tf_op jit(solution)/shard_map/ppermute | solution.py:547
  27.1 8.2 %collective-permute-start.6 = (f32[8,1024]{1,0:T(8,128)S(1)}, f32[8,1024]{1,0:T(8,128)S(1)}, u32[]{:S(2)}, u32[]{:S(2)}) collective-permute-start(f32[8,1024]{1,0:T(8,128)S(1)} %get-tuple-element.24), channel_id=1, source_target_pairs={{0,192},{1,193},{2,194},{3,195},{4,196},{5,197},{6,198},{7,199},{8... | collective-permute-start | bytes 98312 | tf_op jit(solution)/shard_map/ppermute | solution.py:547
  29.0 10.3 %collective-permute-start = (f32[272,128]{1,0:T(8,128)S(1)}, f32[272,128]{1,0:T(8,128)S(1)}, u32[]{:S(2)}, u32[]{:S(2)}) collective-permute-start(f32[272,128]{1,0:T(8,128)S(1)} %get-tuple-element.18), channel_id=1, source_target_pairs={{0,1},{1,0},{2,3},{3,2},{4,5},{5,4},{6,7},{7,6},{8,9},{9,8},{10,11... | collective-permute-start | bytes 417800 | tf_op jit(solution)/shard_map/ppermute | solution.py:555
  32.0 7.3 %collective-permute-start.1 = (f32[272,128]{1,0:T(8,128)S(1)}, f32[272,128]{1,0:T(8,128)S(1)}, u32[]{:S(2)}, u32[]{:S(2)}) collective-permute-start(f32[272,128]{1,0:T(8,128)S(1)} %get-tuple-element.19), channel_id=1, source_target_pairs={{0,3},{1,2},{2,1},{3,0},{4,7},{5,6},{6,5},{7,4},{8,11},{9,10},{10,... | collective-permute-start | bytes 417800 | tf_op jit(solution)/shard_map/ppermute | solution.py:555
  35.3 28.3 %copy-start.6 = (bf16[256,256]{1,0:T(8,128)(2,1)S(1)}, bf16[256,256]{1,0:T(8,128)(2,1)}, u32[]{:S(2)}) copy-start(bf16[256,256]{1,0:T(8,128)(2,1)} %constant.21.clone.block_high) | copy-start | bytes 393220
  35.3 28.3 %copy-start.7 = (bf16[256,256]{1,0:T(8,128)(2,1)S(1)}, bf16[256,256]{1,0:T(8,128)(2,1)}, u32[]{:S(2)}) copy-start(bf16[256,256]{1,0:T(8,128)(2,1)} %constant.22.clone.block_low) | copy-start | bytes 393220
  35.3 10.0 %collective-permute-start.7 = (f32[8,1024]{1,0:T(8,128)S(1)}, f32[8,1024]{1,0:T(8,128)S(1)}, u32[]{:S(2)}, u32[]{:S(2)}) collective-permute-start(f32[8,1024]{1,0:T(8,128)S(1)} %add_add_fusion.3), channel_id=1, source_target_pairs={{0,4},{1,5},{2,6},{3,7},{4,0},{5,1},{6,2},{7,3},{8,12},{9,13},{10,... | collective-permute-start | bytes 98312 | tf_op jit(solution)/shard_map/ppermute | solution.py:547
  37.6 7.8 %collective-permute-start.8 = (f32[8,1024]{1,0:T(8,128)S(1)}, f32[8,1024]{1,0:T(8,128)S(1)}, u32[]{:S(2)}, u32[]{:S(2)}) collective-permute-start(f32[8,1024]{1,0:T(8,128)S(1)} %add_add_fusion.3), channel_id=1, source_target_pairs={{0,8},{1,9},{2,10},{3,11},{4,12},{5,13},{6,14},{7,15},{8,0},{9,1},... | collective-permute-start | bytes 98312 | tf_op jit(solution)/shard_map/ppermute | solution.py:547
  37.8 7.5 %collective-permute-start.9 = (f32[8,1024]{1,0:T(8,128)S(1)}, f32[8,1024]{1,0:T(8,128)S(1)}, u32[]{:S(2)}, u32[]{:S(2)}) collective-permute-start(f32[8,1024]{1,0:T(8,128)S(1)} %add_add_fusion.3), channel_id=1, source_target_pairs={{0,12},{1,13},{2,14},{3,15},{4,8},{5,9},{6,10},{7,11},{8,4},{9,5},... | collective-permute-start | bytes 98312 | tf_op jit(solution)/shard_map/ppermute | solution.py:547
  40.9 22.7 %collective-permute-start.2 = (f32[1088,128]{1,0:T(8,128)S(1)}, f32[1088,128]{1,0:T(8,128)S(1)}, u32[]{:S(2)}, u32[]{:S(2)}) collective-permute-start(f32[1088,128]{1,0:T(8,128)S(1)} %get-tuple-element.20.sent_near), channel_id=1, source_target_pairs={{0,4},{4,0},{8,12},{12,8},{16,20},{20,16},{24,28},{28,24},{32,36},... | collective-permute-start | bytes 1671176 | tf_op jit(solution)/shard_map/ppermute | solution.py:555
  45.3 18.3 %collective-permute-start.3 = (f32[1088,128]{1,0:T(8,128)S(1)}, f32[1088,128]{1,0:T(8,128)S(1)}, u32[]{:S(2)}, u32[]{:S(2)}) collective-permute-start(f32[1088,128]{1,0:T(8,128)S(1)} %get-tuple-element.21.sent_far), channel_id=1, source_target_pairs={{0,252},{4,8},{8,4},{12,16},{16,12},{20,24},{24,20},{28,32},{32,28... | collective-permute-start | bytes 1671176 | tf_op jit(solution)/shard_map/ppermute | solution.py:555
  45.4 3.9 %collective-permute-start.10 = (f32[8,1024]{1,0:T(8,128)S(1)}, f32[8,1024]{1,0:T(8,128)S(1)}, u32[]{:S(2)}, u32[]{:S(2)}) collective-permute-start(f32[8,1024]{1,0:T(8,128)S(1)} %add_add_fusion.2), channel_id=1, source_target_pairs={{0,16},{1,17},{2,18},{3,19},{4,20},{5,21},{6,22},{7,23},{8,24},{9,... | collective-permute-start | bytes 98312 | tf_op jit(solution)/shard_map/ppermute | solution.py:547
  45.8 4.6 %collective-permute-start.11 = (f32[8,1024]{1,0:T(8,128)S(1)}, f32[8,1024]{1,0:T(8,128)S(1)}, u32[]{:S(2)}, u32[]{:S(2)}) collective-permute-start(f32[8,1024]{1,0:T(8,128)S(1)} %add_add_fusion.2), channel_id=1, source_target_pairs={{0,32},{1,33},{2,34},{3,35},{4,36},{5,37},{6,38},{7,39},{8,40},{9,... | collective-permute-start | bytes 98312 | tf_op jit(solution)/shard_map/ppermute | solution.py:547
  47.6 4.8 %collective-permute-start.12 = (f32[8,1024]{1,0:T(8,128)S(1)}, f32[8,1024]{1,0:T(8,128)S(1)}, u32[]{:S(2)}, u32[]{:S(2)}) collective-permute-start(f32[8,1024]{1,0:T(8,128)S(1)} %add_add_fusion.2), channel_id=1, source_target_pairs={{0,48},{1,49},{2,50},{3,51},{4,52},{5,53},{6,54},{7,55},{8,56},{9,... | collective-permute-start | bytes 98312 | tf_op jit(solution)/shard_map/ppermute | solution.py:547
  52.4 5.9 %collective-permute-start.13 = (f32[8,1024]{1,0:T(8,128)S(1)}, f32[8,1024]{1,0:T(8,128)S(1)}, u32[]{:S(2)}, u32[]{:S(2)}) collective-permute-start(f32[8,1024]{1,0:T(8,128)S(1)} %add_add_fusion.1), channel_id=1, source_target_pairs={{0,1},{1,0},{2,3},{3,2},{4,5},{5,4},{6,7},{7,6},{8,9},{9,8},{10,11... | collective-permute-start | bytes 98312 | tf_op jit(solution)/shard_map/ppermute | solution.py:547
  53.8 8.6 %collective-permute-start.14 = (f32[8,1024]{1,0:T(8,128)S(1)}, f32[8,1024]{1,0:T(8,128)S(1)}, u32[]{:S(2)}, u32[]{:S(2)}) collective-permute-start(f32[8,1024]{1,0:T(8,128)S(1)} %add_add_fusion.1), channel_id=1, source_target_pairs={{0,2},{1,3},{2,0},{3,1},{4,6},{5,7},{6,4},{7,5},{8,10},{9,11},{10,... | collective-permute-start | bytes 98312 | tf_op jit(solution)/shard_map/ppermute | solution.py:547
  58.4 5.2 %collective-permute-start.15 = (f32[8,1024]{1,0:T(8,128)S(1)}, f32[8,1024]{1,0:T(8,128)S(1)}, u32[]{:S(2)}, u32[]{:S(2)}) collective-permute-start(f32[8,1024]{1,0:T(8,128)S(1)} %add_add_fusion.1), channel_id=1, source_target_pairs={{0,3},{1,2},{2,1},{3,0},{4,7},{5,6},{6,5},{7,4},{8,11},{9,10},{10,... | collective-permute-start | bytes 98312 | tf_op jit(solution)/shard_map/ppermute | solution.py:547
  73.1 1.5 %copy-start.8 = (f32[40,256]{1,0:T(8,128)S(1)}, f32[40,256]{1,0:T(8,128)}, u32[]{:S(2)}) copy-start(f32[40,256]{1,0:T(8,128)} %constant.23.clone.columns_y) | copy-start | bytes 122884
  (3 other events, 3.7 us)

commit v3 on v2

--- a/solution.py
+++ b/solution.py
@@ -189,7 +189,7 @@
     far[256:272, :] = jnp.where(even, sent[1][1], sent[0][1])
 
 
-def widen_kernel(parity, field, got_near, got_far, near, far, wide):
+def widen_kernel(parity, field, got_near, got_far, wide_far, near, far, wide, sems):
     lane = lanes((512, 128))
     even = parity[0] == 0
     before = jnp.where(even, got_far[...], got_near[...])
@@ -199,6 +199,7 @@
         jnp.concatenate([roll(v[256:272], -32 * q) for q in range(4)], axis=0)
         for v in (before, after)
     ]
+    copies = []
     narrow = lanes((64, 128))
     for ex in range(EXL):
         own = roll(field[:, ex // 2 * 128 : ex // 2 * 128 + 128], 32 - ex % 2 * 64)
@@ -212,6 +213,9 @@
         at = pl.ds(ex * 512, 64, stride=8)
         inside = (narrow >= 112) & (narrow < 120)
         wide[at, :] = jnp.where(inside, roll(faces[1], 112 - 8 * ex), wide[at, :])
+        part = pl.ds(ex * 512, 512)
+        copies.append(pltpu.make_async_copy(wide.at[part], wide_far.at[part], sems.at[ex]))
+        copies[ex].start()
 
     def send(up, down):
         up[0:1024, :] = wide[1024:2048, :]
@@ -221,6 +225,8 @@
 
     pl.when(parity[1] == 0)(lambda: send(near, far))
     pl.when(parity[1] != 0)(lambda: send(far, near))
+    for copy in copies:
+        copy.wait()
 
 
 def pair_step(old, new, base, block_high, block_low):
@@ -284,19 +290,17 @@
 
 
 def first_step_kernel(
-    parity, sent_near, sent_far, got_near, got_far, block_high, block_low,
-    new, features_x, features_z, old, wall,
+    parity, wide, got_near, got_far, block_high, block_low, new, features_x, features_z, old, wall
 ):
-    def place(left, right, up, down):
+    def place(left, right):
         old[448:512, :] = left[1024:1088, :]
         old[512:1536, :] = left[0:1024, :]
-        old[1536:2560, :] = down[0:1024, :]
-        old[2560:3584, :] = up[0:1024, :]
         old[3584:4608, :] = right[0:1024, :]
         old[4608:4672, :] = right[1024:1088, :]
 
-    pl.when(parity[1] == 0)(lambda: place(got_far, got_near, sent_near, sent_far))
-    pl.when(parity[1] != 0)(lambda: place(got_near, got_far, sent_far, sent_near))
+    pl.when(parity[1] == 0)(lambda: place(got_far, got_near))
+    pl.when(parity[1] != 0)(lambda: place(got_near, got_far))
+    old[1536:3584, :] = wide[...]
 
     source = lax.broadcasted_iota(jnp.int32, (256, 128), 0)
     goal = lanes((256, 128)) % 32
@@ -577,14 +581,16 @@
     )
     near, far = swapped(near, far, "group")
     counts = lax.all_to_all(counts, "solver", 0, 0, tiled=True)
-    sent_near, sent_far = call(
+    wide, near, far = call(
         widen_kernel,
-        [sds((1088, 128)), sds((1088, 128))],
-        [pltpu.VMEM((2048, 128), F32)],
+        [sds((2048, 128)), sds((1088, 128)), sds((1088, 128))],
+        [pltpu.VMEM((2048, 128), F32), pltpu.SemaphoreType.DMA((4,))],
         1,
         parity, field, near, far,
+        results=[HB, VM, VM],
+        limit=52500,
     )
-    near, far = swapped(sent_near, sent_far, "solver")
+    near, far = swapped(near, far, "solver")
 
     grad, features = call(
         grad_kernel,
@@ -608,7 +614,7 @@
             u, block_high, block_low,
         )
 
-    for number, shift in enumerate((6, 2, 4, 0)):
+    for number, shift in enumerate((0, 6, 4, 2)):
         got = partners(grad, shift)
         if number == 1:
             u, features_x, features_z = call(
@@ -616,7 +622,7 @@
                 [state, sds((64, 256), BF), sds((64, 256), BF)],
                 [space, pltpu.VMEM((512, 128), F32)],
                 1,
-                parity, sent_near, sent_far, near, far, block_high, block_low,
+                parity, wide, near, far, block_high, block_low,
             )
         if number == 2:
             u = middle(middle(u, 1, 4), 2, 3)

time: 82.1 us -> 82.5 us (level); the launches traced: 81.1 us -> 82.3 us
  starting transfers between devices: 28.5 us -> 25.6 us
  waiting for transfers between devices: 8.35 us -> 10.6 us
  local copies, waits for them, and re-layouts: 0.71 us -> 1.93 us
    ppermute x4, starting transfers between devices: 10.7 us -> 7.78 us  [swapped(): return (lax.ppermute(near, axis, pairs), lax.ppermute(far, axis, others))]
    ppermute x4, waiting for transfers between devices: 0.01 us -> 2.45 us  [swapped(): return (lax.ppermute(near, axis, pairs), lax.ppermute(far, axis, others))]
    unnamed x22 -> x24, local copies, waits for them, and re-layouts: 0.71 us -> 1.93 us
  transfers between devices with their start and end apart: 16 -> 16, of which waited for: 4 -> 4; matrix products, arithmetic and copies ran while one was open for 0% -> 0% of each run, Pallas kernels for 2% -> 3%
where the time goes in v3:
time: 82.5 us; the launch traced here: 82.3 us
  starting transfers between devices  25.6 us (31%)
  Pallas kernels  25.3 us (31%)
  blocking collectives  17.9 us (22%)
  waiting for transfers between devices  10.6 us (13%)
  local copies, waits for them, and re-layouts  1.93 us (2%)
  between operations  0.86 us (1%)
    pallas_call x9, Pallas kernels, call(): pl.pallas_call(kernel, out_shape=out_shape, in_specs=[SM] * scalars + [ar...  25.3 us
    all_to_all x1, blocking collectives, shards(): counts = lax.all_to_all(counts, 'solver', 0, 0, tiled=True)  17.9 us
    ppermute x12, starting transfers between devices, partners(): lax.ppermute(value, both, [(d, d ^ m << shift) for d in range(devices)])  17.8 us
    ppermute x12, waiting for transfers between devices, partners(): lax.ppermute(value, both, [(d, d ^ m << shift) for d in range(devices)])  8.18 us
    ppermute x4, starting transfers between devices, swapped(): return (lax.ppermute(near, axis, pairs), lax.ppermute(far, axis, others))  7.78 us
    ppermute x4, waiting for transfers between devices, swapped(): return (lax.ppermute(near, axis, pairs), lax.ppermute(far, axis, others))  2.45 us
    unnamed x24, local copies, waits for them, and re-layouts  1.93 us
  transfers between devices with their start and end apart: 16, of which 4 were waited for; matrix products, arithmetic and copies ran while one was open for 0% of the time, Pallas kernels for 3%

profile of v3, /device:TPU:1, one launch (start us, length us, event | category | flops | bytes accessed | tf_op | source)
XLA Modules:
  0.0 82.3 jit_solution(12041072896286752518)
XLA Ops:
  1.4 2.3 %shard_map.130 = (f32[64,128]{1,0:T(8,128)S(1)}, f32[272,128]{1,0:T(8,128)S(1)}, f32[272,128]{1,0:T(8,128)S(1)}) custom-call(s32[2]{0:T(128)S(1)} %pad_add_fusion.parity, f32[512,256]{1,0:T(8,128)} %bitcast.14, s32[1,64]{1,0:T(1,128)S(1)} %bitcast.19), custom_call_target="tpu_custom_call" | custom-call | flops 4000000000 | bytes 1000000 | tf_op jit(solution)/shard_map/pallas_call | solution.py:533
  3.7 17.9 %all_to_all.11 = f32[64,1,128]{2,1,0:T(1,128)S(1)} all-to-all(f32[64,1,128]{2,1,0:T(1,128)S(1)} %bitcast.12), channel_id=1, replica_groups=mesh['solver'=64,'group'=4] {'solver'}, dimensions={0} | all-to-all | bytes 65536 | tf_op jit(solution)/shard_map/all_to_all | solution.py:583
  21.6 3.5 %shard_map.131 = (f32[8,1024]{1,0:T(8,128)S(1)}, bf16[64,256]{1,0:T(8,128)(2,1)S(1)}) custom-call(f32[512,256]{1,0:T(8,128)S(1)} %bitcast.15, bf16[8,1024]{1,0:T(8,128)(2,1)S(1)} %copy-done.1, bf16[1,1024]{1,0:T(2,128)(2,1)S(1)} %bitcast.17, s32[2,256]{1,0:T(2,128)S(1)} %copy-done.3, s32[1,64]{1,0:T(1,128)S(1)} %bitcast.20, s32[1,64]{1,0:T(1,128)S(1)} %bitcast.21, ...), custom_call_target="tpu_custom_call" | custom-call | flops 4000000000 | bytes 1000000 | tf_op jit(solution)/shard_map/pallas_call | solution.py:533
  25.1 5.1 %collective-permute-start.6 = (f32[8,1024]{1,0:T(8,128)S(1)}, f32[8,1024]{1,0:T(8,128)S(1)}, u32[]{:S(2)}, u32[]{:S(2)}) collective-permute-start(f32[8,1024]{1,0:T(8,128)S(1)} %get-tuple-element.26), channel_id=1, source_target_pairs={{0,3},{1,2},{2,1},{3,0},{4,7},{5,6},{6,5},{7,4},{8,11},{9,10},{10,... | collective-permute-start | bytes 98312 | tf_op jit(solution)/shard_map/ppermute | solution.py:551
  30.3 1.2 %collective-permute-start.5 = (f32[8,1024]{1,0:T(8,128)S(1)}, f32[8,1024]{1,0:T(8,128)S(1)}, u32[]{:S(2)}, u32[]{:S(2)}) collective-permute-start(f32[8,1024]{1,0:T(8,128)S(1)} %get-tuple-element.26), channel_id=1, source_target_pairs={{0,2},{1,3},{2,0},{3,1},{4,6},{5,7},{6,4},{7,5},{8,10},{9,11},{10,... | collective-permute-start | bytes 98312 | tf_op jit(solution)/shard_map/ppermute | solution.py:551
  32.4 1.3 %collective-permute-start = (f32[272,128]{1,0:T(8,128)S(1)}, f32[272,128]{1,0:T(8,128)S(1)}, u32[]{:S(2)}, u32[]{:S(2)}) collective-permute-start(f32[272,128]{1,0:T(8,128)S(1)} %get-tuple-element.19), channel_id=1, source_target_pairs={{0,1},{1,0},{2,3},{3,2},{4,5},{5,4},{6,7},{7,6},{8,9},{9,8},{10,11... | collective-permute-start | bytes 417800 | tf_op jit(solution)/shard_map/ppermute | solution.py:559
  33.8 3.3 %collective-permute-start.1 = (f32[272,128]{1,0:T(8,128)S(1)}, f32[272,128]{1,0:T(8,128)S(1)}, u32[]{:S(2)}, u32[]{:S(2)}) collective-permute-start(f32[272,128]{1,0:T(8,128)S(1)} %get-tuple-element.20), channel_id=1, source_target_pairs={{0,3},{1,2},{2,1},{3,0},{4,7},{5,6},{6,5},{7,4},{8,11},{9,10},{10,... | collective-permute-start | bytes 417800 | tf_op jit(solution)/shard_map/ppermute | solution.py:559
  38.1 1.4 %collective-permute-start.8 = (f32[8,1024]{1,0:T(8,128)S(1)}, f32[8,1024]{1,0:T(8,128)S(1)}, u32[]{:S(2)}, u32[]{:S(2)}) collective-permute-start(f32[8,1024]{1,0:T(8,128)S(1)} %add_add_fusion.3), channel_id=1, source_target_pairs={{0,128},{1,129},{2,130},{3,131},{4,132},{5,133},{6,134},{7,135},{8... | collective-permute-start | bytes 98312 | tf_op jit(solution)/shard_map/ppermute | solution.py:551
  40.5 2.4 %collective-permute-done.got_near = f32[272,128]{1,0:T(8,128)S(1)} collective-permute-done((f32[272,128]{1,0:T(8,128)S(1)}, f32[272,128]{1,0:T(8,128)S(1)}, u32[]{:S(2)}, u32[]{:S(2)}) %collective-permute-start) | collective-permute-done | bytes 139296 | tf_op jit(solution)/shard_map/ppermute | solution.py:559
  42.9 2.3 %shard_map.132 = (f32[2048,128]{1,0:T(8,128)}, f32[1088,128]{1,0:T(8,128)S(1)}, f32[1088,128]{1,0:T(8,128)S(1)}) custom-call(s32[2]{0:T(128)S(1)} %pad_add_fusion.parity, f32[512,256]{1,0:T(8,128)S(1)} %bitcast.16, f32[272,128]{1,0:T(8,128)S(1)} %collective-permute-done.got_near, f32[272,128]{1,0:T(8,128)S(1)} %collective-permute-done.1.got_far), custom_call_target="tpu_custom_call" | custom-call | flops 4000000000 | bytes 1000000 | tf_op jit(solution)/shard_map/pallas_call | solution.py:533
  45.2 2.7 %collective-permute-start.2 = (f32[1088,128]{1,0:T(8,128)S(1)}, f32[1088,128]{1,0:T(8,128)S(1)}, u32[]{:S(2)}, u32[]{:S(2)}) collective-permute-start(f32[1088,128]{1,0:T(8,128)S(1)} %get-tuple-element.22), channel_id=1, source_target_pairs={{0,4},{4,0},{8,12},{12,8},{16,20},{20,16},{24,28},{28,24},{32,36},... | collective-permute-start | bytes 1671176 | tf_op jit(solution)/shard_map/ppermute | solution.py:559
  48.4 1.0 %collective-permute-start.12 = (f32[8,1024]{1,0:T(8,128)S(1)}, f32[8,1024]{1,0:T(8,128)S(1)}, u32[]{:S(2)}, u32[]{:S(2)}) collective-permute-start(f32[8,1024]{1,0:T(8,128)S(1)} %add_add_fusion.2), channel_id=1, source_target_pairs={{0,48},{1,49},{2,50},{3,51},{4,52},{5,53},{6,54},{7,55},{8,56},{9,... | collective-permute-start | bytes 98312 | tf_op jit(solution)/shard_map/ppermute | solution.py:551
  49.4 1.1 %collective-permute-start.11 = (f32[8,1024]{1,0:T(8,128)S(1)}, f32[8,1024]{1,0:T(8,128)S(1)}, u32[]{:S(2)}, u32[]{:S(2)}) collective-permute-start(f32[8,1024]{1,0:T(8,128)S(1)} %add_add_fusion.2), channel_id=1, source_target_pairs={{0,32},{1,33},{2,34},{3,35},{4,36},{5,37},{6,38},{7,39},{8,40},{9,... | collective-permute-start | bytes 98312 | tf_op jit(solution)/shard_map/ppermute | solution.py:551
  50.5 1.2 %collective-permute-start.10 = (f32[8,1024]{1,0:T(8,128)S(1)}, f32[8,1024]{1,0:T(8,128)S(1)}, u32[]{:S(2)}, u32[]{:S(2)}) collective-permute-start(f32[8,1024]{1,0:T(8,128)S(1)} %add_add_fusion.2), channel_id=1, source_target_pairs={{0,16},{1,17},{2,18},{3,19},{4,20},{5,21},{6,22},{7,23},{8,24},{9,... | collective-permute-start | bytes 98312 | tf_op jit(solution)/shard_map/ppermute | solution.py:551
  52.4 1.6 %collective-permute-done.11 = f32[8,1024]{1,0:T(8,128)S(1)} collective-permute-done((f32[8,1024]{1,0:T(8,128)S(1)}, f32[8,1024]{1,0:T(8,128)S(1)}, u32[]{:S(2)}, u32[]{:S(2)}) %collective-permute-start.11) | collective-permute-done | bytes 32800 | tf_op jit(solution)/shard_map/ppermute | solution.py:551
  54.0 3.2 %collective-permute-start.15 = (f32[8,1024]{1,0:T(8,128)S(1)}, f32[8,1024]{1,0:T(8,128)S(1)}, u32[]{:S(2)}, u32[]{:S(2)}) collective-permute-start(f32[8,1024]{1,0:T(8,128)S(1)} %add_add_fusion.1), channel_id=1, source_target_pairs={{0,12},{1,13},{2,14},{3,15},{4,8},{5,9},{6,10},{7,11},{8,4},{9,5},... | collective-permute-start | bytes 98312 | tf_op jit(solution)/shard_map/ppermute | solution.py:551
  57.8 5.8 %collective-permute-done.15 = f32[8,1024]{1,0:T(8,128)S(1)} collective-permute-done((f32[8,1024]{1,0:T(8,128)S(1)}, f32[8,1024]{1,0:T(8,128)S(1)}, u32[]{:S(2)}, u32[]{:S(2)}) %collective-permute-start.15) | collective-permute-done | bytes 32800 | tf_op jit(solution)/shard_map/ppermute | solution.py:551
  63.7 1.2 %copy-done.11 = f32[2048,128]{1,0:T(8,128)S(1)} copy-done((f32[2048,128]{1,0:T(8,128)S(1)}, f32[2048,128]{1,0:T(8,128)}, u32[]{:S(2)}) %copy-start.11) | copy-done | bytes 1048600
  64.9 3.6 %shard_map.133 = (f32[5120,128]{1,0:T(8,128)S(1)}, bf16[64,256]{1,0:T(8,128)(2,1)S(1)}, bf16[64,256]{1,0:T(8,128)(2,1)S(1)}) custom-call(s32[2]{0:T(128)S(1)} %pad_add_fusion.parity, f32[2048,128]{1,0:T(8,128)S(1)} %copy-done.11, f32[1088,128]{1,0:T(8,128)S(1)} %collective-permute-done.2.got_near, f32[1088,128]{1,0:T(8,128)S(1)} %collective-permute-done.3.got_far, ...), custom_call_target="tpu_custom_call" | custom-call | flops 4000000000 | bytes 1000000 | tf_op jit(solution)/shard_map/pallas_call | solution.py:533
  68.5 2.3 %shard_map.134.old = f32[5120,128]{1,0:T(8,128)S(1)} custom-call(f32[5120,128]{1,0:T(8,128)S(1)} %get-tuple-element.27.old, bf16[256,256]{1,0:T(8,128)(2,1)S(1)} %copy-done.7, bf16[256,256]{1,0:T(8,128)(2,1)S(1)} %copy-done.6), custom_call_target="tpu_custom_call" | custom-call | flops 4000000000 | bytes 1000000 | tf_op jit(solution)/shard_map/pallas_call | solution.py:533
  70.8 1.7 %shard_map.135.old = f32[5120,128]{1,0:T(8,128)S(1)} custom-call(f32[5120,128]{1,0:T(8,128)S(1)} %shard_map.134.old, bf16[256,256]{1,0:T(8,128)(2,1)S(1)} %copy-done.7, bf16[256,256]{1,0:T(8,128)(2,1)S(1)} %copy-done.6), custom_call_target="tpu_custom_call" | custom-call | flops 4000000000 | bytes 1000000 | tf_op jit(solution)/shard_map/pallas_call | solution.py:533
  72.6 1.7 %shard_map.136.old = f32[5120,128]{1,0:T(8,128)S(1)} custom-call(f32[5120,128]{1,0:T(8,128)S(1)} %shard_map.135.old, bf16[256,256]{1,0:T(8,128)(2,1)S(1)} %copy-done.7, bf16[256,256]{1,0:T(8,128)(2,1)S(1)} %copy-done.6), custom_call_target="tpu_custom_call" | custom-call | flops 4000000000 | bytes 1000000 | tf_op jit(solution)/shard_map/pallas_call | solution.py:533
  74.4 1.5 %shard_map.137.u = f32[512,256]{1,0:T(8,128)S(1)} custom-call(f32[5120,128]{1,0:T(8,128)S(1)} %shard_map.136.old, bf16[256,256]{1,0:T(8,128)(2,1)S(1)} %copy-done.7, bf16[256,256]{1,0:T(8,128)(2,1)S(1)} %copy-done.6), custom_call_target="tpu_custom_call" | custom-call | flops 4000000000 | bytes 1000000 | tf_op jit(solution)/shard_map/pallas_call | solution.py:533
  75.9 6.4 %shard_map.138 = (bf16[8,1024]{1,0:T(8,128)(2,1)}, bf16[1,1024]{1,0:T(2,128)(2,1)}, f32[512,256]{1,0:T(8,128)}) custom-call(bf16[8,1024]{1,0:T(8,128)(2,1)S(1)} %copy-done.1, bf16[1,1024]{1,0:T(2,128)(2,1)S(1)} %bitcast.18, s32[2,256]{1,0:T(2,128)S(1)} %copy-done.3, bf16[64,256]{1,0:T(8,128)(2,1)S(1)} %get-tuple-element.18.features_own, ...), custom_call_target="tpu_custom_call" | custom-call | flops 4000000000 | bytes 1000000 | tf_op jit(solution)/shard_map/pallas_call | solution.py:533
  (47 shorter events, 5.6 us)
Async XLA Ops:
  1.4 20.2 %copy-start = (f32[8,8,8,256]{3,2,1,0:T(8,128)S(1)}, f32[8,8,8,256]{3,2,1,0:T(8,128)}, u32[]{:S(2)}) copy-start(f32[8,8,8,256]{3,2,1,0:T(8,128)} %param.11) | copy-start | bytes 1572868
  1.4 20.2 %copy-start.1 = (bf16[8,1024]{1,0:T(8,128)(2,1)S(1)}, bf16[8,1024]{1,0:T(8,128)(2,1)}, u32[]{:S(2)}) copy-start(bf16[8,1024]{1,0:T(8,128)(2,1)} %first.3) | copy-start | bytes 49156
  1.4 20.2 %copy-start.2 = (bf16[1024,1]{0,1:T(2,128)(2,1)S(1)}, bf16[1024,1]{0,1:T(2,128)(2,1)}, u32[]{:S(2)}) copy-start(bf16[1024,1]{0,1:T(2,128)(2,1)} %param.13) | copy-start | bytes 6148
  1.4 20.2 %copy-start.3 = (s32[2,256]{1,0:T(2,128)S(1)}, s32[2,256]{1,0:T(2,128)}, u32[]{:S(2)}) copy-start(s32[2,256]{1,0:T(2,128)} %edges.3) | copy-start | bytes 6148
  1.4 20.2 %copy-start.5 = (s32[64]{0:T(128)S(1)}, s32[64]{0:T(128)}, u32[]{:S(2)}) copy-start(s32[64]{0:T(128)} %param.15) | copy-start | bytes 772
  25.1 12.0 %collective-permute-start.6 = (f32[8,1024]{1,0:T(8,128)S(1)}, f32[8,1024]{1,0:T(8,128)S(1)}, u32[]{:S(2)}, u32[]{:S(2)}) collective-permute-start(f32[8,1024]{1,0:T(8,128)S(1)} %get-tuple-element.26), channel_id=1, source_target_pairs={{0,3},{1,2},{2,1},{3,0},{4,7},{5,6},{6,5},{7,4},{8,11},{9,10},{10,... | collective-permute-start | bytes 98312 | tf_op jit(solution)/shard_map/ppermute | solution.py:551
  30.3 6.9 %collective-permute-start.5 = (f32[8,1024]{1,0:T(8,128)S(1)}, f32[8,1024]{1,0:T(8,128)S(1)}, u32[]{:S(2)}, u32[]{:S(2)}) collective-permute-start(f32[8,1024]{1,0:T(8,128)S(1)} %get-tuple-element.26), channel_id=1, source_target_pairs={{0,2},{1,3},{2,0},{3,1},{4,6},{5,7},{6,4},{7,5},{8,10},{9,11},{10,... | collective-permute-start | bytes 98312 | tf_op jit(solution)/shard_map/ppermute | solution.py:551
  31.4 5.7 %collective-permute-start.4 = (f32[8,1024]{1,0:T(8,128)S(1)}, f32[8,1024]{1,0:T(8,128)S(1)}, u32[]{:S(2)}, u32[]{:S(2)}) collective-permute-start(f32[8,1024]{1,0:T(8,128)S(1)} %get-tuple-element.26), channel_id=1, source_target_pairs={{0,1},{1,0},{2,3},{3,2},{4,5},{5,4},{6,7},{7,6},{8,9},{9,8},{10,11... | collective-permute-start | bytes 98312 | tf_op jit(solution)/shard_map/ppermute | solution.py:551
  32.4 10.5 %collective-permute-start = (f32[272,128]{1,0:T(8,128)S(1)}, f32[272,128]{1,0:T(8,128)S(1)}, u32[]{:S(2)}, u32[]{:S(2)}) collective-permute-start(f32[272,128]{1,0:T(8,128)S(1)} %get-tuple-element.19), channel_id=1, source_target_pairs={{0,1},{1,0},{2,3},{3,2},{4,5},{5,4},{6,7},{7,6},{8,9},{9,8},{10,11... | collective-permute-start | bytes 417800 | tf_op jit(solution)/shard_map/ppermute | solution.py:559
  33.8 9.2 %collective-permute-start.1 = (f32[272,128]{1,0:T(8,128)S(1)}, f32[272,128]{1,0:T(8,128)S(1)}, u32[]{:S(2)}, u32[]{:S(2)}) collective-permute-start(f32[272,128]{1,0:T(8,128)S(1)} %get-tuple-element.20), channel_id=1, source_target_pairs={{0,3},{1,2},{2,1},{3,0},{4,7},{5,6},{6,5},{7,4},{8,11},{9,10},{10,... | collective-permute-start | bytes 417800 | tf_op jit(solution)/shard_map/ppermute | solution.py:559
  37.1 26.6 %copy-start.6 = (bf16[256,256]{1,0:T(8,128)(2,1)S(1)}, bf16[256,256]{1,0:T(8,128)(2,1)}, u32[]{:S(2)}) copy-start(bf16[256,256]{1,0:T(8,128)(2,1)} %constant.22.clone.block_low) | copy-start | bytes 393220
  37.1 26.6 %copy-start.7 = (bf16[256,256]{1,0:T(8,128)(2,1)S(1)}, bf16[256,256]{1,0:T(8,128)(2,1)}, u32[]{:S(2)}) copy-start(bf16[256,256]{1,0:T(8,128)(2,1)} %constant.21.clone.block_high) | copy-start | bytes 393220
  37.1 11.2 %collective-permute-start.9 = (f32[8,1024]{1,0:T(8,128)S(1)}, f32[8,1024]{1,0:T(8,128)S(1)}, u32[]{:S(2)}, u32[]{:S(2)}) collective-permute-start(f32[8,1024]{1,0:T(8,128)S(1)} %add_add_fusion.3), channel_id=1, source_target_pairs={{0,192},{1,193},{2,194},{3,195},{4,196},{5,197},{6,198},{7,199},{8... | collective-permute-start | bytes 98312 | tf_op jit(solution)/shard_map/ppermute | solution.py:551
  38.1 10.3 %collective-permute-start.8 = (f32[8,1024]{1,0:T(8,128)S(1)}, f32[8,1024]{1,0:T(8,128)S(1)}, u32[]{:S(2)}, u32[]{:S(2)}) collective-permute-start(f32[8,1024]{1,0:T(8,128)S(1)} %add_add_fusion.3), channel_id=1, source_target_pairs={{0,128},{1,129},{2,130},{3,131},{4,132},{5,133},{6,134},{7,135},{8... | collective-permute-start | bytes 98312 | tf_op jit(solution)/shard_map/ppermute | solution.py:551
  39.5 8.9 %collective-permute-start.7 = (f32[8,1024]{1,0:T(8,128)S(1)}, f32[8,1024]{1,0:T(8,128)S(1)}, u32[]{:S(2)}, u32[]{:S(2)}) collective-permute-start(f32[8,1024]{1,0:T(8,128)S(1)} %add_add_fusion.3), channel_id=1, source_target_pairs={{0,64},{1,65},{2,66},{3,67},{4,68},{5,69},{6,70},{7,71},{8,72},{9,... | collective-permute-start | bytes 98312 | tf_op jit(solution)/shard_map/ppermute | solution.py:551
  45.2 18.5 %collective-permute-start.2 = (f32[1088,128]{1,0:T(8,128)S(1)}, f32[1088,128]{1,0:T(8,128)S(1)}, u32[]{:S(2)}, u32[]{:S(2)}) collective-permute-start(f32[1088,128]{1,0:T(8,128)S(1)} %get-tuple-element.22), channel_id=1, source_target_pairs={{0,4},{4,0},{8,12},{12,8},{16,20},{20,16},{24,28},{28,24},{32,36},... | collective-permute-start | bytes 1671176 | tf_op jit(solution)/shard_map/ppermute | solution.py:559
  47.9 15.8 %collective-permute-start.3 = (f32[1088,128]{1,0:T(8,128)S(1)}, f32[1088,128]{1,0:T(8,128)S(1)}, u32[]{:S(2)}, u32[]{:S(2)}) collective-permute-start(f32[1088,128]{1,0:T(8,128)S(1)} %get-tuple-element.23), channel_id=1, source_target_pairs={{0,252},{4,8},{8,4},{12,16},{16,12},{20,24},{24,20},{28,32},{32,28... | collective-permute-start | bytes 1671176 | tf_op jit(solution)/shard_map/ppermute | solution.py:559
  48.4 4.1 %collective-permute-start.12 = (f32[8,1024]{1,0:T(8,128)S(1)}, f32[8,1024]{1,0:T(8,128)S(1)}, u32[]{:S(2)}, u32[]{:S(2)}) collective-permute-start(f32[8,1024]{1,0:T(8,128)S(1)} %add_add_fusion.2), channel_id=1, source_target_pairs={{0,48},{1,49},{2,50},{3,51},{4,52},{5,53},{6,54},{7,55},{8,56},{9,... | collective-permute-start | bytes 98312 | tf_op jit(solution)/shard_map/ppermute | solution.py:551
  49.4 4.6 %collective-permute-start.11 = (f32[8,1024]{1,0:T(8,128)S(1)}, f32[8,1024]{1,0:T(8,128)S(1)}, u32[]{:S(2)}, u32[]{:S(2)}) collective-permute-start(f32[8,1024]{1,0:T(8,128)S(1)} %add_add_fusion.2), channel_id=1, source_target_pairs={{0,32},{1,33},{2,34},{3,35},{4,36},{5,37},{6,38},{7,39},{8,40},{9,... | collective-permute-start | bytes 98312 | tf_op jit(solution)/shard_map/ppermute | solution.py:551
  50.5 3.5 %collective-permute-start.10 = (f32[8,1024]{1,0:T(8,128)S(1)}, f32[8,1024]{1,0:T(8,128)S(1)}, u32[]{:S(2)}, u32[]{:S(2)}) collective-permute-start(f32[8,1024]{1,0:T(8,128)S(1)} %add_add_fusion.2), channel_id=1, source_target_pairs={{0,16},{1,17},{2,18},{3,19},{4,20},{5,21},{6,22},{7,23},{8,24},{9,... | collective-permute-start | bytes 98312 | tf_op jit(solution)/shard_map/ppermute | solution.py:551
  54.0 9.6 %collective-permute-start.15 = (f32[8,1024]{1,0:T(8,128)S(1)}, f32[8,1024]{1,0:T(8,128)S(1)}, u32[]{:S(2)}, u32[]{:S(2)}) collective-permute-start(f32[8,1024]{1,0:T(8,128)S(1)} %add_add_fusion.1), channel_id=1, source_target_pairs={{0,12},{1,13},{2,14},{3,15},{4,8},{5,9},{6,10},{7,11},{8,4},{9,5},... | collective-permute-start | bytes 98312 | tf_op jit(solution)/shard_map/ppermute | solution.py:551
  57.2 6.4 %collective-permute-start.14 = (f32[8,1024]{1,0:T(8,128)S(1)}, f32[8,1024]{1,0:T(8,128)S(1)}, u32[]{:S(2)}, u32[]{:S(2)}) collective-permute-start(f32[8,1024]{1,0:T(8,128)S(1)} %add_add_fusion.1), channel_id=1, source_target_pairs={{0,8},{1,9},{2,10},{3,11},{4,12},{5,13},{6,14},{7,15},{8,0},{9,1},... | collective-permute-start | bytes 98312 | tf_op jit(solution)/shard_map/ppermute | solution.py:551
  57.8 5.8 %collective-permute-start.13 = (f32[8,1024]{1,0:T(8,128)S(1)}, f32[8,1024]{1,0:T(8,128)S(1)}, u32[]{:S(2)}, u32[]{:S(2)}) collective-permute-start(f32[8,1024]{1,0:T(8,128)S(1)} %add_add_fusion.1), channel_id=1, source_target_pairs={{0,4},{1,5},{2,6},{3,7},{4,0},{5,1},{6,2},{7,3},{8,12},{9,13},{10,... | collective-permute-start | bytes 98312 | tf_op jit(solution)/shard_map/ppermute | solution.py:551
  74.3 1.5 %copy-start.8 = (f32[40,256]{1,0:T(8,128)S(1)}, f32[40,256]{1,0:T(8,128)}, u32[]{:S(2)}) copy-start(f32[40,256]{1,0:T(8,128)} %constant.23.clone.columns_y) | copy-start | bytes 122884
  (4 other events, 5.0 us)
